TPU v7x, 8 devices: a whole 2x2x1 slice. The times are simulated.
8 devices in a mesh: dp: 1 (over z), tp: 2 (over y), cp: 4 (over x, core).
Axes of the slice: x: 2, y: 2, z: 1, core: 2. Of those that a mesh axis runs over, the one named last changes fastest.
Arguments:
- hidden: bfloat16 [1024, 4096], P(('dp', 'cp'))
- positions: int32 [1024], P(('dp', 'cp'))
- norm_gain: bfloat16 [4096], replicated
- w_query: bfloat16 [4096, 4096], P(None, 'tp')
- w_key: bfloat16 [4096, 1024], P(None, 'tp')
- w_value: bfloat16 [4096, 1024], P(None, 'tp')
- w_out: bfloat16 [4096, 4096], P('tp')
Outputs:
- output 1: bfloat16 [1024, 4096], P(('dp', 'cp'))
- output 2: bfloat16 [1024, 8, 128], P(('dp', 'cp'), 'tp')
- output 3: bfloat16 [1024, 8, 128], P(('dp', 'cp'), 'tp')
All inputs are finite; a program needn't handle non-finite values.
Results may differ from a plain program's by a relative error of at most 0.00808662.
Values are sent between devices in bfloat16 or wider.
A program may use at most 1 GiB of HBM per device.

v0:
```python
import math
import jax
import jax.numpy as jnp
from jax import lax
from jax.sharding import PartitionSpec as P

HEAD = 128
EPS = 1e-5
LOG_THETA = math.log(1000000.0)
SCORE_SCALE = 1.0 / math.sqrt(HEAD)


def rms_norm(hidden, norm_gain):
    hidden_f = hidden.astype(jnp.float32)
    inv_rms = lax.rsqrt(jnp.mean(hidden_f * hidden_f, axis=-1, keepdims=True) + EPS)
    return (hidden_f * inv_rms * norm_gain.astype(jnp.float32)).astype(jnp.bfloat16)


def rope_tables(positions):
    half_dim = HEAD // 2
    inv_freq = jnp.exp(jnp.arange(half_dim, dtype=jnp.float32) * (-2.0 * LOG_THETA / HEAD))
    angles = positions.astype(jnp.float32)[..., None] * inv_freq
    return jnp.cos(angles), jnp.sin(angles)


def apply_rope(head_vals, cos_t, sin_t):
    half_dim = HEAD // 2
    first_half = head_vals[..., :half_dim]
    second_half = head_vals[..., half_dim:]
    return jnp.concatenate([first_half * cos_t - second_half * sin_t, second_half * cos_t + first_half * sin_t], axis=-1)


def project_heads(hidden, positions, norm_gain, w_query, w_key, w_value):
    row_count = hidden.shape[0]
    kv_local = w_key.shape[1] // HEAD
    group_size = w_query.shape[1] // (HEAD * kv_local)
    normed = rms_norm(hidden, norm_gain)
    cos_t, sin_t = rope_tables(positions)
    q_proj = jnp.dot(normed, w_query, preferred_element_type=jnp.float32).reshape(row_count, kv_local, group_size, HEAD)
    queries = apply_rope(q_proj, cos_t[:, None, None, :], sin_t[:, None, None, :]).astype(jnp.bfloat16)
    k_proj = jnp.dot(normed, w_key, preferred_element_type=jnp.float32).reshape(row_count, kv_local, HEAD)
    k_rope = apply_rope(k_proj, cos_t[:, None, :], sin_t[:, None, :]).astype(jnp.bfloat16)
    v_heads = jnp.dot(normed, w_value, preferred_element_type=jnp.float32).astype(jnp.bfloat16).reshape(row_count, kv_local, HEAD)
    return queries, k_rope, v_heads


def own_block_stats(queries, k_rope, v_heads, positions):
    scores = jnp.einsum('uohf,tof->ohut', queries, k_rope, preferred_element_type=jnp.float32) * SCORE_SCALE
    visible = positions[None, :] <= positions[:, None]
    scores = jnp.where(visible, scores, -jnp.inf)
    run_max = jnp.max(scores, axis=-1)
    weights = jnp.exp(scores - run_max[..., None])
    run_sum = jnp.sum(weights, axis=-1)
    acc_out = jnp.einsum('ohut,tof->ohuf', weights.astype(jnp.bfloat16), v_heads, preferred_element_type=jnp.float32)
    return run_max, run_sum, acc_out


def attend_block(queries, kv_blk, soft_stats):
    run_max, run_sum, acc_out = soft_stats
    scores = jnp.einsum('uohf,tof->ohut', queries, kv_blk[0], preferred_element_type=jnp.float32) * SCORE_SCALE
    new_max = jnp.maximum(run_max, jnp.max(scores, axis=-1))
    rescale = jnp.exp(run_max - new_max)
    weights = jnp.exp(scores - new_max[..., None])
    new_sum = run_sum * rescale + jnp.sum(weights, axis=-1)
    new_acc = acc_out * rescale[..., None] + jnp.einsum('ohut,tof->ohuf', weights.astype(jnp.bfloat16), kv_blk[1], preferred_element_type=jnp.float32)
    return new_max, new_sum, new_acc


def output_sum(hidden, soft_stats, w_out):
    run_max, run_sum, acc_out = soft_stats
    attn_o = (acc_out / run_sum[..., None]).astype(jnp.bfloat16)
    w_out_r = w_out.reshape(acc_out.shape[0], acc_out.shape[1], HEAD, hidden.shape[1])
    part_sum = jnp.einsum('ngte,ngef->tf', attn_o, w_out_r, preferred_element_type=jnp.float32).astype(jnp.bfloat16)
    attn_sum = lax.psum(part_sum, 'tp')
    return (hidden.astype(jnp.float32) + attn_sum.astype(jnp.float32)).astype(jnp.bfloat16)


def solution(mesh):
    blocks = mesh.shape['cp']
    shift_pairs = [(src_idx, (src_idx + 1) % blocks) for src_idx in range(blocks)]
    row_spec = P(('dp', 'cp'), None)
    cache_spec = P(('dp', 'cp'), 'tp', None)
    head_cols = P(None, 'tp')

    def local_block(hidden, positions, norm_gain, w_query, w_key, w_value, w_out):
        my_block = lax.axis_index('cp')
        queries, k_rope, v_heads = project_heads(hidden, positions, norm_gain, w_query, w_key, w_value)
        soft_stats = own_block_stats(queries, k_rope, v_heads, positions)

        def shift_step(step_idx, loop_carry):
            kv_blk, stats_in = loop_carry
            kv_blk = lax.ppermute(kv_blk, 'cp', shift_pairs)

            def take_block(state_in):
                return attend_block(queries, kv_blk, state_in)

            def keep_stats(state_in):
                return state_in

            stats_out = lax.cond(step_idx <= my_block, take_block, keep_stats, stats_in)
            return kv_blk, stats_out

        kv_own = jnp.stack([k_rope, v_heads])
        _, soft_stats = lax.fori_loop(1, blocks, shift_step, (kv_own, soft_stats))
        return output_sum(hidden, soft_stats, w_out), k_rope, v_heads

    return jax.shard_map(local_block, mesh=mesh, in_specs=(row_spec, P(('dp', 'cp')), P(None), head_cols, head_cols, head_cols, P('tp', None)), out_specs=(row_spec, cache_spec, cache_spec), check_vma=False)
```

profile of v0, /device:TPU:3, one launch (start us, length us, event | category | flops | bytes accessed | tf_op | source)
XLA Modules:
  0.0 158.6 jit_solution(17000968168110457539)
XLA Ops:
  9.5 2.1 %fusion.23 = f32[256]{0:T(256)S(1)} fusion(bf16[256,4096]{1,0:T(8,128)(2,1)} %param.11), kind=kLoop, calls=%fused_computation.24 | loop fusion | flops 3145472 | bytes 2098176 | tf_op jit(solution)/shard_map/reduce_sum | solution.py:15
  11.6 4.3 %convolution_convert_fusion = bf16[256,512]{1,0:T(8,128)(2,1)S(1)} fusion(bf16[4096,512]{1,0:T(8,128)(2,1)} %param.16, bf16[256,4096]{1,0:T(8,128)(2,1)} %param.11, f32[4096]{0:T(1024)S(1)} %convert_element_type.51, f32[256]{0:T(256)S(1)} %add_rsqrt_fusion), kind=kOutput, calls=%fused_computation.41 | convolution fusion | flops 1078067200 | bytes 6571008 | tf_op jit(solution)/shard_map/dot_general | solution.py:43
  16.7 3.5 %fusion.45 = f32[256,512]{1,0:T(8,128)S(1)} fusion(bf16[4096,512]{1,0:T(8,128)(2,1)} %param.15, bf16[256,4096]{1,0:T(8,128)(2,1)S(1)} %copy-done.1, f32[4096]{0:T(1024)S(1)} %convert_element_type.51, f32[256]{0:T(256)S(1)} %add_rsqrt_fusion), kind=kOutput, calls=%fused_computation.59 | convolution fusion | flops 1077936128 | bytes 6833152 | tf_op jit(solution)/shard_map/dot_general | solution.py:41
  21.5 9.5 %fusion.42 = f32[256,2048]{1,0:T(8,128)} fusion(bf16[4096,2048]{1,0:T(8,128)(2,1)} %param.14, bf16[256,4096]{1,0:T(8,128)(2,1)S(1)} %copy-done.1, f32[4096]{0:T(1024)S(1)} %convert_element_type.51, f32[256]{0:T(256)S(1)} %add_rsqrt_fusion), kind=kOutput, calls=%fused_computation.58 | convolution fusion | flops 4299161600 | bytes 20988928 | tf_op jit(solution)/shard_map/dot_general | solution.py:39
  31.0 2.7 %reshape.158 = f32[256,4,4,128]{3,2,1,0:T(4,128)S(1)} reshape(f32[256,2048]{1,0:T(8,128)} %fusion.42) | data formatting | bytes 4194304 | tf_op jit(solution)/shard_map/reshape | solution.py:39
  33.7 1.4 fusion.47
  36.0 1.4 subtract_convert_fusion
  40.6 1.3 fusion.30
  42.9 35.4 %while.19 = (s32[]{:T(128)}, bf16[2,256,4,128]{3,1,2,0:T(8,128)(2,1)}, f32[4,4,256]{2,1,0:T(4,128)S(1)}, f32[4,4,256]{2,1,0:T(4,128)S(1)}, f32[4,4,256,128]{3,2,...) while((s32[]{:T(128)}, bf16[2,256,4,128]{3,1,2,0:T(8,128)(2,1)}, ...), condition=%wide.region_8.9_spmd, body=%wide.region_3.8_spmd.sunk | while | flops 546316288 | bytes 21758188 | solution.py:104
  42.9 6.1 %collective-permute-done = bf16[2,256,4,128]{3,1,2,0:T(8,128)(2,1)S(1)} collective-permute-done((bf16[2,256,4,128]{3,1,2,0:T(8,128)(2,1)}, bf16[2,256,4,128]{3,1,2,0:T(8,128)(2,1)S(1)}, u32[]{:S(2)}, u32[]{:S(2)}) %collective-permute-start) | collective-permute-done | bytes 524320 | tf_op jit(solution)/shard_map/while/body/eval_jaxpr/ppermute | solution.py:92
  49.0 4.6 %conditional.2 = ((f32[4,4,256]{2,1,0:T(4,128)S(1)}, f32[4,4,256]{2,1,0:T(4,128)S(1)}, f32[4,4,256,128]{3,2,1,0:T(8,128)S(1)})) conditional(s32[]{:T(128)} %convert_element_type.92, (f32[4,4,256]{2,1,0:T(4,128)S(1)}, f32[4,4,256]{2,1,0:T(4,128)S(1)}, f32[4,4,256,128]{3,2,1,0:T(8,128)S(1)}) %tuple.51, (bf16[2,256,4,128]{3,1,2,0:T(8,128)(2,1)S(1)}, ...), branch_computations={%region_4.4_spmd, %region_5.7_spmd} | conditional | flops 546316288 | bytes 18612256 | solution.py:100
  49.0 1.9 %bitcast_reduce_fusion = (f32[4,4,256]{2,1,0:T(4,128)S(1)}, f32[4,256,256,4]{2,1,3,0:T(8,128)S(1)}) fusion(bf16[256,4,4,128]{3,0,2,1:T(8,128)(2,1)} %get-tuple-element.139, bf16[2,256,4,128]{3,1,2,0:T(8,128)(2,1)S(1)} %get-tuple-element.138), kind=kOutput, calls=%fused_computation.1 | convolution fusion | flops 270528512 | bytes 5521408 | tf_op jit(solution)/shard_map/while/body/eval_jaxpr/cond/branch_1_fun/uohf,tof->ohut/dot_general | solution.py:60
  51.7 1.8 %multiply_add_fusion = f32[4,4,256,128]{3,2,1,0:T(8,128)S(1)} fusion(f32[4,4,256,128]{3,2,1,0:T(8,128)S(1)} %get-tuple-element.141, f32[4,256,256,4]{2,1,3,0:T(8,128)S(1)} %get-tuple-element.180, f32[4,4,256]{2,1,0:T(4,128)S(1)} %max.2, f32[4,4,256]{2,1,0:T(4,128)S(1)} %bitcast.67, bf16[2,256,4,128]{3,1,2,0:T(8,128)(2,1)S(1)} %get-tuple-element.138), kind=kOutput, calls=%fused_computation.6 | convolution fusion | flops 272629760 | bytes 8683520 | tf_op jit(solution)/shard_map/while/body/eval_jaxpr/cond/branch_1_fun/ohut,tof->ohuf/dot_general | solution.py:65
  54.4 6.1 %collective-permute-done = bf16[2,256,4,128]{3,1,2,0:T(8,128)(2,1)S(1)} collective-permute-done((bf16[2,256,4,128]{3,1,2,0:T(8,128)(2,1)}, bf16[2,256,4,128]{3,1,2,0:T(8,128)(2,1)S(1)}, u32[]{:S(2)}, u32[]{:S(2)}) %collective-permute-start) | collective-permute-done | bytes 524320 | tf_op jit(solution)/shard_map/while/body/eval_jaxpr/ppermute | solution.py:92
  60.5 4.6 %conditional.2 = ((f32[4,4,256]{2,1,0:T(4,128)S(1)}, f32[4,4,256]{2,1,0:T(4,128)S(1)}, f32[4,4,256,128]{3,2,1,0:T(8,128)S(1)})) conditional(s32[]{:T(128)} %convert_element_type.92, (f32[4,4,256]{2,1,0:T(4,128)S(1)}, f32[4,4,256]{2,1,0:T(4,128)S(1)}, f32[4,4,256,128]{3,2,1,0:T(8,128)S(1)}) %tuple.51, (bf16[2,256,4,128]{3,1,2,0:T(8,128)(2,1)S(1)}, ...), branch_computations={%region_4.4_spmd, %region_5.7_spmd} | conditional | flops 546316288 | bytes 18612256 | solution.py:100
  60.5 1.9 %bitcast_reduce_fusion = (f32[4,4,256]{2,1,0:T(4,128)S(1)}, f32[4,256,256,4]{2,1,3,0:T(8,128)S(1)}) fusion(bf16[256,4,4,128]{3,0,2,1:T(8,128)(2,1)} %get-tuple-element.139, bf16[2,256,4,128]{3,1,2,0:T(8,128)(2,1)S(1)} %get-tuple-element.138), kind=kOutput, calls=%fused_computation.1 | convolution fusion | flops 270528512 | bytes 5521408 | tf_op jit(solution)/shard_map/while/body/eval_jaxpr/cond/branch_1_fun/uohf,tof->ohut/dot_general | solution.py:60
  63.2 1.8 %multiply_add_fusion = f32[4,4,256,128]{3,2,1,0:T(8,128)S(1)} fusion(f32[4,4,256,128]{3,2,1,0:T(8,128)S(1)} %get-tuple-element.141, f32[4,256,256,4]{2,1,3,0:T(8,128)S(1)} %get-tuple-element.180, f32[4,4,256]{2,1,0:T(4,128)S(1)} %max.2, f32[4,4,256]{2,1,0:T(4,128)S(1)} %bitcast.67, bf16[2,256,4,128]{3,1,2,0:T(8,128)(2,1)S(1)} %get-tuple-element.138), kind=kOutput, calls=%fused_computation.6 | convolution fusion | flops 272629760 | bytes 8683520 | tf_op jit(solution)/shard_map/while/body/eval_jaxpr/cond/branch_1_fun/ohut,tof->ohuf/dot_general | solution.py:65
  65.9 7.1 %collective-permute-done = bf16[2,256,4,128]{3,1,2,0:T(8,128)(2,1)S(1)} collective-permute-done((bf16[2,256,4,128]{3,1,2,0:T(8,128)(2,1)}, bf16[2,256,4,128]{3,1,2,0:T(8,128)(2,1)S(1)}, u32[]{:S(2)}, u32[]{:S(2)}) %collective-permute-start) | collective-permute-done | bytes 524320 | tf_op jit(solution)/shard_map/while/body/eval_jaxpr/ppermute | solution.py:92
  73.0 4.6 %conditional.2 = ((f32[4,4,256]{2,1,0:T(4,128)S(1)}, f32[4,4,256]{2,1,0:T(4,128)S(1)}, f32[4,4,256,128]{3,2,1,0:T(8,128)S(1)})) conditional(s32[]{:T(128)} %convert_element_type.92, (f32[4,4,256]{2,1,0:T(4,128)S(1)}, f32[4,4,256]{2,1,0:T(4,128)S(1)}, f32[4,4,256,128]{3,2,1,0:T(8,128)S(1)}) %tuple.51, (bf16[2,256,4,128]{3,1,2,0:T(8,128)(2,1)S(1)}, ...), branch_computations={%region_4.4_spmd, %region_5.7_spmd} | conditional | flops 546316288 | bytes 18612256 | solution.py:100
  73.0 1.9 %bitcast_reduce_fusion = (f32[4,4,256]{2,1,0:T(4,128)S(1)}, f32[4,256,256,4]{2,1,3,0:T(8,128)S(1)}) fusion(bf16[256,4,4,128]{3,0,2,1:T(8,128)(2,1)} %get-tuple-element.139, bf16[2,256,4,128]{3,1,2,0:T(8,128)(2,1)S(1)} %get-tuple-element.138), kind=kOutput, calls=%fused_computation.1 | convolution fusion | flops 270528512 | bytes 5521408 | tf_op jit(solution)/shard_map/while/body/eval_jaxpr/cond/branch_1_fun/uohf,tof->ohut/dot_general | solution.py:60
  75.7 1.8 %multiply_add_fusion = f32[4,4,256,128]{3,2,1,0:T(8,128)S(1)} fusion(f32[4,4,256,128]{3,2,1,0:T(8,128)S(1)} %get-tuple-element.141, f32[4,256,256,4]{2,1,3,0:T(8,128)S(1)} %get-tuple-element.180, f32[4,4,256]{2,1,0:T(4,128)S(1)} %max.2, f32[4,4,256]{2,1,0:T(4,128)S(1)} %bitcast.67, bf16[2,256,4,128]{3,1,2,0:T(8,128)(2,1)S(1)} %get-tuple-element.138), kind=kOutput, calls=%fused_computation.6 | convolution fusion | flops 272629760 | bytes 8683520 | tf_op jit(solution)/shard_map/while/body/eval_jaxpr/cond/branch_1_fun/ohut,tof->ohuf/dot_general | solution.py:65
  78.3 9.2 %fusion.20 = bf16[256,4096]{1,0:T(8,128)(2,1)} fusion(bf16[4,4,128,4096]{3,2,1,0:T(8,128)(2,1)} %bitcast.72, f32[4,4,256,128]{3,2,1,0:T(8,128)S(1)} %get-tuple-element.158, f32[4,4,256]{2,1,0:T(4,128)S(1)} %get-tuple-element.159), kind=kOutput, calls=%fused_computation.23 | convolution fusion | flops 4297064448 | bytes 20987904 | tf_op jit(solution)/shard_map/ngte,ngef->tf/dot_general | solution.py:73
  88.4 59.0 %all-reduce.2.cloned.1.call-done = bf16[256,4096]{1,0:T(8,128)(2,1)} async-done(((bf16[256,4096]{1,0:T(8,128)(2,1)}), bf16[256,4096]{1,0:T(8,128)(2,1)}) %all-reduce.2.cloned.1.call-update) | async-done | bytes 2097168 | tf_op jit(solution)/shard_map/psum | solution.py:74
  147.4 4.3 %fusion.26 = bf16[256,4096]{1,0:T(8,128)(2,1)} fusion(bf16[256,4096]{1,0:T(8,128)(2,1)} %param.11, bf16[256,4096]{1,0:T(8,128)(2,1)} %all-reduce.2.cloned.1.call-done), kind=kLoop, calls=%fused_computation.27 | loop fusion | flops 4194304 | bytes 6291456 | tf_op jit(solution)/shard_map/convert_element_type | solution.py:75
  (48 shorter events, 15.0 us)
Async XLA Ops:
  7.2 140.3 %all-reduce.2.cloned.1.call-start = ((), (), s32[]{:S(2)}) async-start(), calls=%async_computation | async-start | bytes 4194304 | tf_op jit(solution)/shard_map/psum | solution.py:74
  11.6 5.1 %copy-start.1 = (bf16[256,4096]{1,0:T(8,128)(2,1)S(1)}, bf16[256,4096]{1,0:T(8,128)(2,1)}, u32[]{:S(2)}) copy-start(bf16[256,4096]{1,0:T(8,128)(2,1)} %param.11) | copy-start | bytes 6291460
  15.9 24.7 %copy-start.3 = (bf16[256,4,128]{2,1,0:T(4,128)(2,1)}, bf16[256,4,128]{2,1,0:T(4,128)(2,1)S(1)}, u32[]{:S(2)}) copy-start(bf16[256,4,128]{2,1,0:T(4,128)(2,1)S(1)} %reshape.159) | copy-start | bytes 786436
  33.7 2.0 %copy-start.2 = (f32[256,4,64]{2,1,0:T(4,128)S(1)}, f32[256,4,64]{2,1,0:T(4,128)}, u32[]{:S(2)}) copy-start(f32[256,4,64]{2,1,0:T(4,128)} %get-tuple-element.188) | copy-start | bytes 786436
  37.9 1.0 copy-start
  40.6 1.4 copy-start.4
  42.9 6.1 %collective-permute-start = (bf16[2,256,4,128]{3,1,2,0:T(8,128)(2,1)}, bf16[2,256,4,128]{3,1,2,0:T(8,128)(2,1)S(1)}, u32[]{:S(2)}, u32[]{:S(2)}) collective-permute-start(bf16[2,256,4,128]{3,1,2,0:T(8,128)(2,1)} %get-tuple-element.259), channel_id=1, source_target_pairs={{0,1},{1,2},{2,3},{3,0},{4,5},{5,6},{6,7},{7,4}} | collective-permute-start | bytes 1572872 | tf_op jit(solution)/shard_map/while/body/eval_jaxpr/ppermute | solution.py:92
  54.4 6.1 %collective-permute-start = (bf16[2,256,4,128]{3,1,2,0:T(8,128)(2,1)}, bf16[2,256,4,128]{3,1,2,0:T(8,128)(2,1)S(1)}, u32[]{:S(2)}, u32[]{:S(2)}) collective-permute-start(bf16[2,256,4,128]{3,1,2,0:T(8,128)(2,1)} %get-tuple-element.259), channel_id=1, source_target_pairs={{0,1},{1,2},{2,3},{3,0},{4,5},{5,6},{6,7},{7,4}} | collective-permute-start | bytes 1572872 | tf_op jit(solution)/shard_map/while/body/eval_jaxpr/ppermute | solution.py:92
  65.9 7.1 %collective-permute-start = (bf16[2,256,4,128]{3,1,2,0:T(8,128)(2,1)}, bf16[2,256,4,128]{3,1,2,0:T(8,128)(2,1)S(1)}, u32[]{:S(2)}, u32[]{:S(2)}) collective-permute-start(bf16[2,256,4,128]{3,1,2,0:T(8,128)(2,1)} %get-tuple-element.259), channel_id=1, source_target_pairs={{0,1},{1,2},{2,3},{3,0},{4,5},{5,6},{6,7},{7,4}} | collective-permute-start | bytes 1572872 | tf_op jit(solution)/shard_map/while/body/eval_jaxpr/ppermute | solution.py:92
Sparse Core Ops, SparseCore 0:
  87.6 59.7 all-reduce.1
where the time goes:
time: 161 us; the launch traced here: 159 us
  waiting for transfers between devices  78.3 us (49%)
  matrix products  39.8 us (25%)
  other arithmetic  15.5 us (10%)
  between operations  14.2 us (9%)
  local copies, waits for them, and re-layouts  10.6 us (7%)
    psum x1, waiting for transfers between devices, output_sum(): attn_sum = lax.psum(part_sum, 'tp')  59 us
    ppermute x3, waiting for transfers between devices, shift_step(): kv_blk = lax.ppermute(kv_blk, 'cp', shift_pairs)  19.3 us
    dot_general x1, matrix products, project_heads(): jnp.dot(normed, w_query, preferred_element_type=jnp.float32)  9.51 us
    dot_general x1, matrix products, output_sum(): jnp.einsum('ngte,ngef->tf', attn_o, w_out_r, preferred_element_type=jnp.f...  9.16 us
    dot_general x3, matrix products, attend_block(): jnp.einsum('uohf,tof->ohut', queries, kv_blk[0], preferred_element_type=j...  5.84 us
    dot_general x3, matrix products, attend_block(): jnp.einsum('ohut,tof->ohuf', weights.astype(jnp.bfloat16), kv_blk[1], pre...  5.53 us
    convert_element_type x1, other arithmetic, output_sum(): (hidden.astype(jnp.float32) + attn_sum.astype(jnp.float32)).astype(jnp.bf...  4.32 us
    dot_general x1, matrix products, project_heads(): jnp.dot(normed, w_value, preferred_element_type=jnp.float32)  4.26 us
  transfers between devices with their start and end apart: 4, of which 4 were waited for; matrix products, arithmetic and copies ran while one was open for 1% of the time, Pallas kernels for 0%

commit v1 on v0

v1 whole, which is shorter than its diff:
```python
import functools
import math

import jax
import jax.numpy as jnp
from jax import lax
from jax.experimental import pallas as pl
from jax.experimental.pallas import tpu as pltpu
from jax.sharding import PartitionSpec as P

HEAD = 128
HALF = HEAD // 2
EPS = 1e-5
LOG_THETA = math.log(1000000.0)
SCORE_SCALE = 1.0 / math.sqrt(HEAD)
EXP2_SCALE = SCORE_SCALE / math.log(2.0)
MESH = pl.DeviceIdType.MESH
ROWS = 256
WIDTH = 4096
KV = 4
GROUP = 4
QCOLS = GROUP * HEAD
OCHUNK = 256
NOUT = WIDTH // OCHUNK
X_PARTS = 4
X_ROWS = ROWS // X_PARTS
NORM_ROWS = 16
F32 = jnp.float32
BF16 = jnp.bfloat16


def copies(refs):
    (x_hbm, pos_hbm, g_hbm, wq_hbm, wk_hbm, wv_hbm, wo_hbm, x_v, pos_v, g_v, wkv_v, wq_v, wo_v, x_sem, small_sem, wkv_sem, wq_sem, wo_sem) = refs

    def x_part(i):
        return pltpu.make_async_copy(x_hbm.at[pl.ds(i * X_ROWS, X_ROWS)], x_v.at[pl.ds(i * X_ROWS, X_ROWS)], x_sem.at[i])

    def wk_part(h):
        return pltpu.make_async_copy(wk_hbm.at[:, pl.ds(h * HEAD, HEAD)], wkv_v.at[h, :, pl.ds(0, HEAD)], wkv_sem.at[0, h])

    def wv_part(h):
        return pltpu.make_async_copy(wv_hbm.at[:, pl.ds(h * HEAD, HEAD)], wkv_v.at[h, :, pl.ds(HEAD, HEAD)], wkv_sem.at[1, h])

    def wq_part(j):
        return pltpu.make_async_copy(wq_hbm.at[:, pl.ds(j * QCOLS, QCOLS)], wq_v.at[j], wq_sem.at[j])

    def wo_part(n):
        cols = pl.ds(pl.multiple_of(n * OCHUNK, OCHUNK), OCHUNK)
        return pltpu.make_async_copy(wo_hbm.at[:, cols], wo_v.at[n], wo_sem.at[n])

    pos_copy = pltpu.make_async_copy(pos_hbm, pos_v, small_sem.at[0])
    g_copy = pltpu.make_async_copy(g_hbm, g_v, small_sem.at[1])
    return x_part, wk_part, wv_part, wq_part, wo_part, pos_copy, g_copy


def rope_tables(pos_v, cos_v, sin_v):
    lane = lax.broadcasted_iota(jnp.int32, (1, HEAD), 1)
    inv_freq = jnp.exp(lax.rem(lane, HALF).astype(F32) * (-2.0 * LOG_THETA / HEAD))
    low = lane < HALF
    top = jnp.broadcast_to(pos_v[pl.ds(0, HEAD)].reshape(1, HEAD).astype(F32), (HEAD, HEAD)).T
    bottom = jnp.broadcast_to(pos_v[pl.ds(HEAD, HEAD)].reshape(1, HEAD).astype(F32), (HEAD, HEAD)).T
    angles = jnp.where(low, top, bottom) * inv_freq
    cos_t, sin_t = jnp.cos(angles), jnp.sin(angles)
    cos_r, sin_r = pltpu.roll(cos_t, HALF, 1), pltpu.roll(sin_t, HALF, 1)
    cos_v[pl.ds(0, HEAD)] = jnp.where(low, cos_t, cos_r)
    cos_v[pl.ds(HEAD, HEAD)] = jnp.where(low, cos_r, cos_t)
    sin_v[pl.ds(0, HEAD)] = jnp.where(low, -sin_t, sin_r)
    sin_v[pl.ds(HEAD, HEAD)] = jnp.where(low, -sin_r, sin_t)


def rope(vals, cos_t, sin_t):
    return vals * cos_t + pltpu.roll(vals, HALF, 1) * sin_t


def attend(blocks, h, q_v, kv_v, o_v):
    row = lax.broadcasted_iota(jnp.int32, (ROWS, ROWS), 0)
    col = lax.broadcasted_iota(jnp.int32, (ROWS, ROWS), 1)
    for g in range(GROUP):
        q = q_v[h, pl.ds(g * ROWS, ROWS), :]
        scores = []
        for b in range(blocks):
            s = lax.dot_general(q, kv_v[b, h, :, pl.ds(0, HEAD)], (((1,), (1,)), ((), ())), preferred_element_type=F32)
            if b == blocks - 1:
                s = jnp.where(col <= row, s, -jnp.inf)
            scores.append(s)
        top = functools.reduce(jnp.maximum, [jnp.max(s, axis=-1, keepdims=True) for s in scores])
        base = top * EXP2_SCALE
        acc, total = None, None
        for b, s in enumerate(scores):
            p = jnp.exp2(s * EXP2_SCALE - base)
            part = jnp.sum(p, axis=-1, keepdims=True)
            pv = jnp.dot(p.astype(BF16), kv_v[b, h, :, pl.ds(HEAD, HEAD)], preferred_element_type=F32)
            total = part if total is None else total + part
            acc = pv if acc is None else acc + pv
        o_v[h, :, pl.ds(g * HEAD, HEAD)] = (acc / total).astype(BF16)


def kernel(x_hbm, pos_hbm, g_hbm, wq_hbm, wk_hbm, wv_hbm, wo_hbm,
           out_v, k_out, v_out,
           x_v, pos_v, g_v, wkv_v, wq_v, wo_v, h_v, cos_v, sin_v, kv_v, q_v, o_v, precv,
           x_sem, small_sem, wkv_sem, wq_sem, wo_sem, kv_send, kv_fwd, kv_recv, p_send, p_recv):
    tp, cp = lax.axis_index("tp"), lax.axis_index("cp")
    other = 1 - tp
    barrier = pltpu.get_barrier_semaphore()
    for t in range(2):
        for c in range(4):
            @pl.when((tp != t) | (cp != c))
            def _():
                pl.semaphore_signal(barrier, inc=1, device_id={"tp": t, "cp": c}, device_id_type=MESH)

    x_part, wk_part, wv_part, wq_part, wo_part, pos_copy, g_copy = copies(
        (x_hbm, pos_hbm, g_hbm, wq_hbm, wk_hbm, wv_hbm, wo_hbm, x_v, pos_v, g_v, wkv_v, wq_v, wo_v, x_sem, small_sem, wkv_sem, wq_sem, wo_sem))

    def start_wkv(h):
        wk_part(h).start()
        wv_part(h).start()

    pos_copy.start()
    g_copy.start()
    for i in range(X_PARTS):
        x_part(i).start()
    start_wkv(0)
    start_wkv(1)

    pos_copy.wait()
    rope_tables(pos_v, cos_v, sin_v)
    g_copy.wait()

    for i in range(X_PARTS):
        x_part(i).wait()

        def square(step, carry):
            rows = pl.ds(pl.multiple_of(i * X_ROWS + step * NORM_ROWS, NORM_ROWS), NORM_ROWS)
            xf = x_v[rows, :].astype(F32)
            mean = jnp.sum(xf * xf, axis=-1, keepdims=True) * (1.0 / WIDTH)
            inv = lax.rsqrt(mean + EPS)
            gain = g_v[...].reshape(1, WIDTH).astype(F32)
            h_v[rows, :] = (xf * inv * gain).astype(BF16)
            return carry

        lax.fori_loop(0, X_ROWS // NORM_ROWS, square, 0)
    start_wkv(2)
    start_wkv(3)

    pl.semaphore_wait(barrier, 7)

    def kv_copy(src_block, h, target, send):
        return pltpu.make_async_remote_copy(
            src_ref=kv_v.at[src_block, h], dst_ref=kv_v.at[src_block, h], send_sem=send.at[h],
            recv_sem=kv_recv.at[src_block, h], device_id={"cp": target}, device_id_type=MESH)

    def own_to(me, target, send, h):
        return kv_copy(me, h, target, send)

    cos_t, sin_t = cos_v[...], sin_v[...]
    hidden = h_v[...]
    for h in range(KV):
        wk_part(h).wait()
        wv_part(h).wait()
        wq_part(h).start()
        kv = jnp.dot(hidden, wkv_v[h], preferred_element_type=F32)
        k = rope(kv[:, :HEAD], cos_v[...], sin_v[...]).astype(BF16)
        v = kv[:, HEAD:].astype(BF16)
        kv_v[cp, h, :, pl.ds(0, HEAD)] = k
        kv_v[cp, h, :, pl.ds(HEAD, HEAD)] = v
        k_out[:, pl.ds(h * HEAD, HEAD)] = k
        v_out[:, pl.ds(h * HEAD, HEAD)] = v

        @pl.when(cp == 0)
        def _():
            own_to(0, 2, kv_send, h).start()
            own_to(0, 1, kv_fwd, h).start()

        @pl.when(cp == 1)
        def _():
            own_to(1, 3, kv_send, h).start()

        @pl.when(cp == 2)
        def _():
            own_to(2, 3, kv_send, h).start()

    def forward(h):
        @pl.when(cp == 2)
        def _():
            kv_copy(0, h, 2, kv_send).wait_recv()
            kv_copy(0, h, 3, kv_fwd).start()

        @pl.when(cp == 3)
        def _():
            kv_copy(1, h, 3, kv_send).wait_recv()
            kv_copy(1, h, 2, kv_fwd).start()

    for j in range(KV):
        wq_part(j).wait()
        for n in range(4):
            wo_part(j * 4 + n).start()
        qp = jnp.dot(hidden, wq_v[j], preferred_element_type=F32)
        for g in range(GROUP):
            q_v[j, pl.ds(g * ROWS, ROWS), :] = rope(qp[:, g * HEAD:(g + 1) * HEAD], cos_v[...], sin_v[...]).astype(BF16)
        if j >= 2:
            forward(j - 2)

    def arrive(src_block, h):
        kv_copy(src_block, h, 0, kv_send).wait_recv()

    @pl.when(cp == 0)
    def _():
        @pl.loop(0, KV)
        def _(h):
            attend(1, h, q_v, kv_v, o_v)

    @pl.when(cp == 1)
    def _():
        @pl.loop(0, KV)
        def _(h):
            arrive(0, h)
            attend(2, h, q_v, kv_v, o_v)

    @pl.when(cp == 2)
    def _():
        @pl.loop(0, KV)
        def _(h):
            arrive(1, h)
            attend(3, h, q_v, kv_v, o_v)

            @pl.when(h < 2)
            def _():
                kv_copy(0, h + 2, 2, kv_send).wait_recv()
                kv_copy(0, h + 2, 3, kv_fwd).start()

    @pl.when(cp == 3)
    def _():
        @pl.loop(0, KV)
        def _(h):
            arrive(0, h)
            arrive(2, h)
            attend(4, h, q_v, kv_v, o_v)

            @pl.when(h < 2)
            def _():
                kv_copy(1, h + 2, 3, kv_send).wait_recv()
                kv_copy(1, h + 2, 2, kv_fwd).start()

    def sent(n):
        return wkv_v.at[0, pl.ds(pl.multiple_of(n * ROWS, ROWS), ROWS), :]

    def p_copy(n):
        return pltpu.make_async_remote_copy(
            src_ref=sent(n), dst_ref=precv.at[n], send_sem=p_send.at[n], recv_sem=p_recv.at[n],
            device_id={"tp": other}, device_id_type=MESH)

    @pl.loop(0, NOUT)
    def _(n):
        wo_part(n).wait()
        part = None
        for h in range(KV):
            d = jnp.dot(o_v[h], wo_v[n, pl.ds(h * QCOLS, QCOLS), :], preferred_element_type=F32)
            part = d if part is None else part + d
        sent(n)[...] = part.astype(BF16)
        p_copy(n).start()

    @pl.loop(0, NOUT)
    def _(n):
        p_copy(n).wait_recv()
        cols = pl.ds(pl.multiple_of(n * OCHUNK, OCHUNK), OCHUNK)
        total = sent(n)[...].astype(F32) + precv[n].astype(F32)
        out_v[:, cols] = (x_v[:, cols].astype(F32) + total).astype(BF16)

    @pl.loop(0, NOUT)
    def _(n):
        p_copy(n).wait_send()

    @pl.loop(0, KV)
    def _(h):
        @pl.when(cp < 3)
        def _():
            kv_copy(0, h, 0, kv_send).wait_send()

        @pl.when((cp == 0) | (cp >= 2))
        def _():
            kv_copy(0, h, 0, kv_fwd).wait_send()


def solution(mesh):
    row_spec = P(('dp', 'cp'), None)
    cache_spec = P(('dp', 'cp'), 'tp', None)
    head_cols = P(None, 'tp')

    def local_block(hidden, positions, norm_gain, w_query, w_key, w_value, w_out):
        dma = pltpu.SemaphoreType.DMA
        out, k_rope, v_heads = pl.pallas_call(
            kernel,
            out_shape=[
                jax.ShapeDtypeStruct((ROWS, WIDTH), BF16),
                jax.ShapeDtypeStruct((ROWS, KV * HEAD), BF16),
                jax.ShapeDtypeStruct((ROWS, KV * HEAD), BF16),
            ],
            in_specs=[pl.BlockSpec(memory_space=pltpu.HBM)] * 7,
            out_specs=[pl.BlockSpec(memory_space=pltpu.VMEM)] * 3,
            scratch_shapes=[
                pltpu.VMEM((ROWS, WIDTH), BF16),
                pltpu.VMEM((ROWS,), jnp.int32),
                pltpu.VMEM((WIDTH,), BF16),
                pltpu.VMEM((KV, WIDTH, 2 * HEAD), BF16),
                pltpu.VMEM((KV, WIDTH, QCOLS), BF16),
                pltpu.VMEM((NOUT, KV * QCOLS, OCHUNK), BF16),
                pltpu.VMEM((ROWS, WIDTH), BF16),
                pltpu.VMEM((ROWS, HEAD), F32),
                pltpu.VMEM((ROWS, HEAD), F32),
                pltpu.VMEM((4, KV, ROWS, 2 * HEAD), BF16),
                pltpu.VMEM((KV, GROUP * ROWS, HEAD), BF16),
                pltpu.VMEM((KV, ROWS, QCOLS), BF16),
                pltpu.VMEM((NOUT, ROWS, OCHUNK), BF16),
                dma((X_PARTS,)), dma((2,)), dma((2, KV)), dma((KV,)), dma((NOUT,)),
                dma((KV,)), dma((KV,)), dma((4, KV)), dma((NOUT,)), dma((NOUT,)),
            ],
            compiler_params=pltpu.CompilerParams(collective_id=0, has_side_effects=True, vmem_limit_bytes=59 << 20),
        )(hidden, positions, norm_gain, w_query, w_key, w_value, w_out)
        return out, k_rope.reshape(ROWS, KV, HEAD), v_heads.reshape(ROWS, KV, HEAD)

    return jax.shard_map(local_block, mesh=mesh, in_specs=(row_spec, P(('dp', 'cp')), P(None), head_cols, head_cols, head_cols, P('tp', None)), out_specs=(row_spec, cache_spec, cache_spec), check_vma=False)
```

time: 161 us -> 81.4 us (0.51); the launches traced: 159 us -> 81.3 us
  waiting for transfers between devices: 78.3 us -> 0 us
  Pallas kernels: 0 us -> 74 us
  matrix products: 39.8 us -> 0 us
  other arithmetic: 15.5 us -> 0 us
  between operations: 14.2 us -> 0.64 us
  local copies, waits for them, and re-layouts: 10.6 us -> 6.56 us
    pallas_call x0 -> x1, Pallas kernels: none -> 74 us  [local_block(): pl.pallas_call(kernel, out_shape=[jax.ShapeDtypeStruct((ROWS, WIDTH), BF1...]
    psum x1 -> x0, waiting for transfers between devices: 59 us -> none  [output_sum(): attn_sum = lax.psum(part_sum, 'tp')]
    dot_general x12 -> x0, matrix products: 39.8 us -> none  [the longest x1 9.51 us: project_heads(): jnp.dot(normed, w_query, preferred_element_type=jnp.float32)]
    ppermute x3 -> x0, waiting for transfers between devices: 19.3 us -> none  [shift_step(): kv_blk = lax.ppermute(kv_blk, 'cp', shift_pairs)]
    convert_element_type x3 -> x0, other arithmetic: 5.71 us -> none  [the longest x1 4.32 us: output_sum(): (hidden.astype(jnp.float32) + attn_sum.astype(jnp.float32)).astype(jnp.bf...]
    reduce_sum x5 -> x0, other arithmetic: 5.17 us -> none  [the longest x3 2.18 us: attend_block(): new_sum = run_sum * rescale + jnp.sum(weights, axis=-1)]
    slice x2 -> x0, local copies, waits for them, and re-layouts: 2.55 us -> none  [apply_rope(): first_half = head_vals[..., :half_dim]]
    another operation x3 -> x0, other arithmetic: 2.45 us -> none
  transfers between devices with their start and end apart: 4 -> 0, of which waited for: 4 -> 0; matrix products, arithmetic and copies ran while one was open for 1% -> 0% of each run, Pallas kernels for 0% -> 0%
where the time goes in v1:
time: 81.4 us; the launch traced here: 81.3 us
  Pallas kernels  74 us (91%)
  local copies, waits for them, and re-layouts  6.56 us (8%)
    pallas_call x1, Pallas kernels, local_block(): pl.pallas_call(kernel, out_shape=[jax.ShapeDtypeStruct((ROWS, WIDTH), BF1...  74 us
    unnamed x1, local copies, waits for them, and re-layouts  3.13 us
    reshape x1, local copies, waits for them, and re-layouts, local_block(): k_rope.reshape(ROWS, KV, HEAD)  1.72 us
    reshape x1, local copies, waits for them, and re-layouts, local_block(): v_heads.reshape(ROWS, KV, HEAD)  1.72 us

profile of v1, /device:TPU:3, one launch (start us, length us, event | category | flops | bytes accessed | tf_op | source)
XLA Modules:
  0.0 81.3 jit_solution(2418816224479229913)
XLA Ops:
  0.6 74.0 %shard_map.94 = (bf16[256,4096]{1,0:T(8,128)(2,1)}, bf16[256,512]{1,0:T(8,128)(2,1)}, bf16[256,512]{1,0:T(8,128)(2,1)}) custom-call(bf16[256,4096]{1,0:T(8,128)(2,1)} %x_hbm.1, s32[256]{0:T(256)} %pos_hbm.1, bf16[4096]{0:T(1024)(128)(2,1)} %g_hbm.1, bf16[4096,2048]{1,0:T(8,128)(2,1)} %wq_hbm.1, bf16[4096,512]{1,0:T(8,128)(2,1)} %wk_hbm.1, ...), custom_call_target="tpu_custom_call" | custom-call | tf_op jit(solution)/shard_map/pallas_call | solution.py:291
  74.7 1.7 %reshape.12 = bf16[256,4,128]{2,1,0:T(4,128)(2,1)} reshape(bf16[256,512]{1,0:T(8,128)(2,1)} %get-tuple-element.7) | data formatting | bytes 524288 | tf_op jit(solution)/shard_map/reshape | solution.py:319
  76.4 1.7 %reshape.13 = bf16[256,4,128]{2,1,0:T(4,128)(2,1)} reshape(bf16[256,512]{1,0:T(8,128)(2,1)} %get-tuple-element.8) | data formatting | bytes 524288 | tf_op jit(solution)/shard_map/reshape | solution.py:319
  78.1 3.1 %copy.11 = bf16[256,4096]{1,0:T(8,128)(2,1)} copy(bf16[256,4096]{1,0:T(8,128)(2,1)} %get-tuple-element.12) | data formatting | bytes 4194304

commit v2 on v1

--- a/solution.py
+++ b/solution.py
@@ -29,8 +29,15 @@
 BF16 = jnp.bfloat16
 
 
+def wo_room(wq_v, n):
+    deep = KV * QCOLS
+    row = pl.multiple_of(lax.rem(n, 4) // 2 * deep, deep)
+    col = pl.multiple_of(lax.rem(n, 2) * OCHUNK, OCHUNK)
+    return wq_v.at[n // 4, pl.ds(row, deep), pl.ds(col, OCHUNK)]
+
+
 def copies(refs):
-    (x_hbm, pos_hbm, g_hbm, wq_hbm, wk_hbm, wv_hbm, wo_hbm, x_v, pos_v, g_v, wkv_v, wq_v, wo_v, x_sem, small_sem, wkv_sem, wq_sem, wo_sem) = refs
+    (x_hbm, pos_hbm, g_hbm, wq_hbm, wk_hbm, wv_hbm, wo_hbm, x_v, pos_v, g_v, wkv_v, wq_v, x_sem, small_sem, wkv_sem, wq_sem, wo_sem) = refs
 
     def x_part(i):
         return pltpu.make_async_copy(x_hbm.at[pl.ds(i * X_ROWS, X_ROWS)], x_v.at[pl.ds(i * X_ROWS, X_ROWS)], x_sem.at[i])
@@ -46,7 +53,7 @@
 
     def wo_part(n):
         cols = pl.ds(pl.multiple_of(n * OCHUNK, OCHUNK), OCHUNK)
-        return pltpu.make_async_copy(wo_hbm.at[:, cols], wo_v.at[n], wo_sem.at[n])
+        return pltpu.make_async_copy(wo_hbm.at[:, cols], wo_room(wq_v, n), wo_sem.at[n])
 
     pos_copy = pltpu.make_async_copy(pos_hbm, pos_v, small_sem.at[0])
     g_copy = pltpu.make_async_copy(g_hbm, g_v, small_sem.at[1])
@@ -97,7 +104,7 @@
 
 def kernel(x_hbm, pos_hbm, g_hbm, wq_hbm, wk_hbm, wv_hbm, wo_hbm,
            out_v, k_out, v_out,
-           x_v, pos_v, g_v, wkv_v, wq_v, wo_v, h_v, cos_v, sin_v, kv_v, q_v, o_v, precv,
+           pos_v, g_v, wkv_v, wq_v, h_v, cos_v, sin_v, kv_v, q_v, o_v, precv, cache_v,
            x_sem, small_sem, wkv_sem, wq_sem, wo_sem, kv_send, kv_fwd, kv_recv, p_send, p_recv):
     tp, cp = lax.axis_index("tp"), lax.axis_index("cp")
     other = 1 - tp
@@ -109,7 +116,7 @@
                 pl.semaphore_signal(barrier, inc=1, device_id={"tp": t, "cp": c}, device_id_type=MESH)
 
     x_part, wk_part, wv_part, wq_part, wo_part, pos_copy, g_copy = copies(
-        (x_hbm, pos_hbm, g_hbm, wq_hbm, wk_hbm, wv_hbm, wo_hbm, x_v, pos_v, g_v, wkv_v, wq_v, wo_v, x_sem, small_sem, wkv_sem, wq_sem, wo_sem))
+        (x_hbm, pos_hbm, g_hbm, wq_hbm, wk_hbm, wv_hbm, wo_hbm, out_v, pos_v, g_v, wkv_v, wq_v, x_sem, small_sem, wkv_sem, wq_sem, wo_sem))
 
     def start_wkv(h):
         wk_part(h).start()
@@ -131,7 +138,7 @@
 
         def square(step, carry):
             rows = pl.ds(pl.multiple_of(i * X_ROWS + step * NORM_ROWS, NORM_ROWS), NORM_ROWS)
-            xf = x_v[rows, :].astype(F32)
+            xf = out_v[rows, :].astype(F32)
             mean = jnp.sum(xf * xf, axis=-1, keepdims=True) * (1.0 / WIDTH)
             inv = lax.rsqrt(mean + EPS)
             gain = g_v[...].reshape(1, WIDTH).astype(F32)
@@ -163,8 +170,6 @@
         v = kv[:, HEAD:].astype(BF16)
         kv_v[cp, h, :, pl.ds(0, HEAD)] = k
         kv_v[cp, h, :, pl.ds(HEAD, HEAD)] = v
-        k_out[:, pl.ds(h * HEAD, HEAD)] = k
-        v_out[:, pl.ds(h * HEAD, HEAD)] = v
 
         @pl.when(cp == 0)
         def _():
@@ -192,11 +197,11 @@
 
     for j in range(KV):
         wq_part(j).wait()
-        for n in range(4):
-            wo_part(j * 4 + n).start()
         qp = jnp.dot(hidden, wq_v[j], preferred_element_type=F32)
         for g in range(GROUP):
             q_v[j, pl.ds(g * ROWS, ROWS), :] = rope(qp[:, g * HEAD:(g + 1) * HEAD], cos_v[...], sin_v[...]).astype(BF16)
+        for n in range(4):
+            wo_part(j * 4 + n).start()
         if j >= 2:
             forward(j - 2)
 
@@ -252,19 +257,25 @@
     @pl.loop(0, NOUT)
     def _(n):
         wo_part(n).wait()
+        room = wo_room(wq_v, n)
         part = None
         for h in range(KV):
-            d = jnp.dot(o_v[h], wo_v[n, pl.ds(h * QCOLS, QCOLS), :], preferred_element_type=F32)
+            d = jnp.dot(o_v[h], room[pl.ds(h * QCOLS, QCOLS), :], preferred_element_type=F32)
             part = d if part is None else part + d
         sent(n)[...] = part.astype(BF16)
         p_copy(n).start()
+
+    for cache, lanes in ((k_out, pl.ds(0, HEAD)), (v_out, pl.ds(HEAD, HEAD))):
+        for h in range(KV):
+            cache_v[pl.ds(h, ROWS, stride=KV), :] = kv_v[cp, h, :, lanes].astype(F32)
+        cache[...] = cache_v[...].astype(BF16)
 
     @pl.loop(0, NOUT)
     def _(n):
         p_copy(n).wait_recv()
         cols = pl.ds(pl.multiple_of(n * OCHUNK, OCHUNK), OCHUNK)
         total = sent(n)[...].astype(F32) + precv[n].astype(F32)
-        out_v[:, cols] = (x_v[:, cols].astype(F32) + total).astype(BF16)
+        out_v[:, cols] = (out_v[:, cols].astype(F32) + total).astype(BF16)
 
     @pl.loop(0, NOUT)
     def _(n):
@@ -279,6 +290,14 @@
         @pl.when((cp == 0) | (cp >= 2))
         def _():
             kv_copy(0, h, 0, kv_fwd).wait_send()
+
+
+def store_results(out_v, k_v, v_v, out_hbm, k_hbm, v_hbm, sem):
+    stores = [pltpu.make_async_copy(src, dst, sem.at[i]) for i, (src, dst) in enumerate(((out_v, out_hbm), (k_v, k_hbm), (v_v, v_hbm)))]
+    for store in stores:
+        store.start()
+    for store in stores:
+        store.wait()
 
 
 def solution(mesh):
@@ -292,18 +311,16 @@
             kernel,
             out_shape=[
                 jax.ShapeDtypeStruct((ROWS, WIDTH), BF16),
-                jax.ShapeDtypeStruct((ROWS, KV * HEAD), BF16),
-                jax.ShapeDtypeStruct((ROWS, KV * HEAD), BF16),
+                jax.ShapeDtypeStruct((ROWS * KV, HEAD), BF16),
+                jax.ShapeDtypeStruct((ROWS * KV, HEAD), BF16),
             ],
             in_specs=[pl.BlockSpec(memory_space=pltpu.HBM)] * 7,
             out_specs=[pl.BlockSpec(memory_space=pltpu.VMEM)] * 3,
             scratch_shapes=[
-                pltpu.VMEM((ROWS, WIDTH), BF16),
                 pltpu.VMEM((ROWS,), jnp.int32),
                 pltpu.VMEM((WIDTH,), BF16),
                 pltpu.VMEM((KV, WIDTH, 2 * HEAD), BF16),
                 pltpu.VMEM((KV, WIDTH, QCOLS), BF16),
-                pltpu.VMEM((NOUT, KV * QCOLS, OCHUNK), BF16),
                 pltpu.VMEM((ROWS, WIDTH), BF16),
                 pltpu.VMEM((ROWS, HEAD), F32),
                 pltpu.VMEM((ROWS, HEAD), F32),
@@ -311,11 +328,20 @@
                 pltpu.VMEM((KV, GROUP * ROWS, HEAD), BF16),
                 pltpu.VMEM((KV, ROWS, QCOLS), BF16),
                 pltpu.VMEM((NOUT, ROWS, OCHUNK), BF16),
+                pltpu.VMEM((ROWS * KV, HEAD), F32),
                 dma((X_PARTS,)), dma((2,)), dma((2, KV)), dma((KV,)), dma((NOUT,)),
                 dma((KV,)), dma((KV,)), dma((4, KV)), dma((NOUT,)), dma((NOUT,)),
             ],
-            compiler_params=pltpu.CompilerParams(collective_id=0, has_side_effects=True, vmem_limit_bytes=59 << 20),
-        )(hidden, positions, norm_gain, w_query, w_key, w_value, w_out)
+            compiler_params=pltpu.CompilerParams(collective_id=0, has_side_effects=True, vmem_limit_bytes=48 << 20),
+        )(*(pltpu.with_memory_space_constraint(a, pltpu.HBM) for a in (hidden, positions, norm_gain, w_query, w_key, w_value, w_out)))
+        out, k_rope, v_heads = pl.pallas_call(
+            store_results,
+            out_shape=[jax.ShapeDtypeStruct(a.shape, BF16) for a in (out, k_rope, v_heads)],
+            in_specs=[pl.BlockSpec(memory_space=pltpu.VMEM)] * 3,
+            out_specs=[pl.BlockSpec(memory_space=pl.ANY)] * 3,
+            scratch_shapes=[dma((3,))],
+            compiler_params=pltpu.CompilerParams(vmem_limit_bytes=4 << 20),
+        )(out, k_rope, v_heads)
         return out, k_rope.reshape(ROWS, KV, HEAD), v_heads.reshape(ROWS, KV, HEAD)
 
     return jax.shard_map(local_block, mesh=mesh, in_specs=(row_spec, P(('dp', 'cp')), P(None), head_cols, head_cols, head_cols, P('tp', None)), out_specs=(row_spec, cache_spec, cache_spec), check_vma=False)

time: 81.4 us -> 74.9 us (0.920)
  local copies, waits for them, and re-layouts: 6.56 us -> 0 us
    reshape x2 -> x0, local copies, waits for them, and re-layouts: 3.43 us -> none  [the longest x1 1.72 us: local_block(): k_rope.reshape(ROWS, KV, HEAD)]
    unnamed x1 -> x0, local copies, waits for them, and re-layouts: 3.13 us -> none
    pallas_call x1, Pallas kernels: 74 us -> 72.5 us  [local_block(): pl.pallas_call(kernel, out_shape=[jax.ShapeDtypeStruct((ROWS, WIDTH), BF1...]
    pallas_call x0 -> x1, Pallas kernels: none -> 1.51 us  [local_block(): pl.pallas_call(store_results, out_shape=[jax.ShapeDtypeStruct(a.shape, BF...]
where the time goes in v2:
time: 74.9 us; the launch traced here: 74.8 us
  Pallas kernels  74 us (99%)
  between operations  0.8 us (1%)
    pallas_call x1, Pallas kernels, local_block(): pl.pallas_call(kernel, out_shape=[jax.ShapeDtypeStruct((ROWS, WIDTH), BF1...  72.5 us
    pallas_call x1, Pallas kernels, local_block(): pl.pallas_call(store_results, out_shape=[jax.ShapeDtypeStruct(a.shape, BF...  1.51 us

profile of v2, /device:TPU:3, one launch (start us, length us, event | category | flops | bytes accessed | tf_op | source)
XLA Modules:
  0.0 74.8 jit_solution(13170146591888592831)
XLA Ops:
  0.6 72.5 %shard_map.94 = (bf16[256,4096]{1,0:T(8,128)(2,1)S(1)}, bf16[1024,128]{1,0:T(8,128)(2,1)S(1)}, bf16[1024,128]{1,0:T(8,128)(2,1)S(1)}) custom-call(bf16[256,4096]{1,0:T(8,128)(2,1)} %x_hbm.1, s32[256]{0:T(256)} %pos_hbm.1, bf16[4096]{0:T(1024)(128)(2,1)} %g_hbm.1, bf16[4096,2048]{1,0:T(8,128)(2,1)} %wq_hbm.1, bf16[4096,512]{1,0:T(8,128)(2,1)} %wk_hbm.1, ...), custom_call_target="tpu_custom_call" | custom-call | tf_op jit(solution)/shard_map/pallas_call | solution.py:310
  73.2 1.5 %shard_map.95 = (bf16[256,4096]{1,0:T(8,128)(2,1)}, bf16[1024,128]{1,0:T(8,128)(2,1)}, bf16[1024,128]{1,0:T(8,128)(2,1)}) custom-call(bf16[256,4096]{1,0:T(8,128)(2,1)S(1)} %get-tuple-element.9.out_v, bf16[1024,128]{1,0:T(8,128)(2,1)S(1)} %get-tuple-element.10.k_v, bf16[1024,128]{1,0:T(8,128)(2,1)S(1)} %get-tuple-element.11.v_v), custom_call_target="tpu_custom_call" | custom-call | tf_op jit(solution)/shard_map/pallas_call | solution.py:337

commit v3 on v2

v3 whole, which is shorter than its diff:
```python
import functools
import math

import jax
import jax.numpy as jnp
from jax import lax
from jax.experimental import pallas as pl
from jax.experimental.pallas import tpu as pltpu
from jax.sharding import PartitionSpec as P

HEAD = 128
HALF = HEAD // 2
EPS = 1e-5
LOG_THETA = math.log(1000000.0)
SCORE_SCALE = 1.0 / math.sqrt(HEAD)
EXP2_SCALE = SCORE_SCALE / math.log(2.0)
MESH = pl.DeviceIdType.MESH
ROWS = 256
WIDTH = 4096
KV = 4
GROUP = 4
QCOLS = GROUP * HEAD
PAIR = 2 * HEAD
OCHUNK = 256
NOUT = WIDTH // OCHUNK
X_PARTS = 4
X_ROWS = ROWS // X_PARTS
NORM_COLS = 1024
SLICES = WIDTH // NORM_COLS
RELAY_STEP = 6
LAG = 3
DETOURS = 2
F32 = jnp.float32
BF16 = jnp.bfloat16


def wo_room(wq_v, n):
    deep = KV * QCOLS
    row = pl.multiple_of(lax.rem(n, 4) // 2 * deep, deep)
    col = pl.multiple_of(lax.rem(n, 2) * OCHUNK, OCHUNK)
    return wq_v.at[n // 4, pl.ds(row, deep), pl.ds(col, OCHUNK)]


def copies(refs):
    (x_hbm, pos_hbm, g_hbm, wq_hbm, wk_hbm, wv_hbm, wo_hbm, x_v, pos_v, g_v, wkv_v, wq_v, x_sem, small_sem, first_sem, wkv_sem, wq_sem, wo_sem) = refs

    def x_part(i):
        return pltpu.make_async_copy(x_hbm.at[pl.ds(i * X_ROWS, X_ROWS)], x_v.at[pl.ds(i * X_ROWS, X_ROWS)], x_sem.at[i])

    def wkv_slice(t):
        rows = pl.ds(t * NORM_COLS, NORM_COLS)
        return [pltpu.make_async_copy(w.at[rows, pl.ds(0, PAIR)], wkv_v.at[0, rows, pl.ds(a * PAIR, PAIR)], first_sem.at[a, t]) for a, w in enumerate((wk_hbm, wv_hbm))]

    def wk_part(i):
        return pltpu.make_async_copy(wk_hbm.at[:, pl.ds(i * PAIR, PAIR)], wkv_v.at[i, :, pl.ds(0, PAIR)], wkv_sem.at[0, i])

    def wv_part(i):
        return pltpu.make_async_copy(wv_hbm.at[:, pl.ds(i * PAIR, PAIR)], wkv_v.at[i, :, pl.ds(PAIR, PAIR)], wkv_sem.at[1, i])

    def wq_part(j):
        return pltpu.make_async_copy(wq_hbm.at[:, pl.ds(j * QCOLS, QCOLS)], wq_v.at[j], wq_sem.at[j])

    def wo_part(n):
        cols = pl.ds(pl.multiple_of(n * OCHUNK, OCHUNK), OCHUNK)
        return pltpu.make_async_copy(wo_hbm.at[:, cols], wo_room(wq_v, n), wo_sem.at[n])

    pos_copy = pltpu.make_async_copy(pos_hbm, pos_v, small_sem.at[0])
    g_copy = pltpu.make_async_copy(g_hbm, g_v, small_sem.at[1])
    return x_part, wkv_slice, wk_part, wv_part, wq_part, wo_part, pos_copy, g_copy


def rope_tables(pos_v, cos_v, sin_v):
    lane = lax.broadcasted_iota(jnp.int32, (1, HEAD), 1)
    inv_freq = jnp.exp(lax.rem(lane, HALF).astype(F32) * (-2.0 * LOG_THETA / HEAD))
    low = lane < HALF
    top = jnp.broadcast_to(pos_v[pl.ds(0, HEAD)].reshape(1, HEAD).astype(F32), (HEAD, HEAD)).T
    bottom = jnp.broadcast_to(pos_v[pl.ds(HEAD, HEAD)].reshape(1, HEAD).astype(F32), (HEAD, HEAD)).T
    angles = jnp.where(low, top, bottom) * inv_freq
    cos_t, sin_t = jnp.cos(angles), jnp.sin(angles)
    cos_r, sin_r = pltpu.roll(cos_t, HALF, 1), pltpu.roll(sin_t, HALF, 1)
    cos_v[pl.ds(0, HEAD)] = jnp.where(low, cos_t, cos_r)
    cos_v[pl.ds(HEAD, HEAD)] = jnp.where(low, cos_r, cos_t)
    sin_v[pl.ds(0, HEAD)] = jnp.where(low, -sin_t, sin_r)
    sin_v[pl.ds(HEAD, HEAD)] = jnp.where(low, -sin_r, sin_t)


def rope(vals, cos_t, sin_t):
    return vals * cos_t + pltpu.roll(vals, HALF, 1) * sin_t


def block_scores(b, h, q_v, kv_v):
    return lax.dot_general(kv_v[b, h, :, pl.ds(0, HEAD)], q_v[h], (((1,), (1,)), ((), ())), preferred_element_type=F32) * EXP2_SCALE


def weighted(weights, b, h, kv_v):
    return lax.dot_general(kv_v[b, h, :, pl.ds(HEAD, HEAD)], weights.astype(BF16), (((0,), (0,)), ((), ())), preferred_element_type=F32)


def store_heads(acc, total, h, o_v):
    vals = (acc / total).astype(BF16)
    for g in range(GROUP):
        o_v[h, :, pl.ds(g * HEAD, HEAD)] = vals[:, g * ROWS:(g + 1) * ROWS].T


def attend_own(me, h, q_v, kv_v, o_v, max_v, sum_v, acc_v):
    key = lax.broadcasted_iota(jnp.int32, (ROWS, GROUP * ROWS), 0)
    query = lax.rem(lax.broadcasted_iota(jnp.int32, (ROWS, GROUP * ROWS), 1), ROWS)
    scores = jnp.where(key <= query, block_scores(me, h, q_v, kv_v), -jnp.inf)
    top = jnp.max(scores, axis=0, keepdims=True)
    weights = jnp.exp2(scores - top)
    total = jnp.sum(weights, axis=0, keepdims=True)
    acc = weighted(weights, me, h, kv_v)
    max_v[h], sum_v[h], acc_v[h] = top, total, acc
    store_heads(acc, total, h, o_v)


def attend_earlier(first, end, last, h, q_v, kv_v, o_v, max_v, sum_v, acc_v):
    scores = [block_scores(b, h, q_v, kv_v) for b in range(first, end)]
    top = functools.reduce(jnp.maximum, [jnp.max(s, axis=0, keepdims=True) for s in scores], max_v[h])
    scale = jnp.exp2(max_v[h] - top)
    total, acc = sum_v[h] * scale, acc_v[h] * scale
    for b, s in enumerate(scores):
        weights = jnp.exp2(s - top)
        total = total + jnp.sum(weights, axis=0, keepdims=True)
        acc = acc + weighted(weights, first + b, h, kv_v)
    if last:
        store_heads(acc, total, h, o_v)
    else:
        max_v[h], sum_v[h], acc_v[h] = top, total, acc


def kernel(x_hbm, pos_hbm, g_hbm, wq_hbm, wk_hbm, wv_hbm, wo_hbm,
           out_v, k_out, v_out,
           pos_v, g_v, wkv_v, wq_v, h_v, gain_v, inv_v, cos_v, sin_v, kv_v, q_v, o_v, max_v, sum_v, acc_v, precv, relay_v, cache_v,
           x_sem, small_sem, first_sem, wkv_sem, wq_sem, wo_sem, kv_send, kv_fwd, kv_recv, p_send, p_recv, relay_send, relay_recv):
    tp, cp = lax.axis_index("tp"), lax.axis_index("cp")
    other = 1 - tp
    x_part, wkv_slice, wk_part, wv_part, wq_part, wo_part, pos_copy, g_copy = copies(
        (x_hbm, pos_hbm, g_hbm, wq_hbm, wk_hbm, wv_hbm, wo_hbm, out_v, pos_v, g_v, wkv_v, wq_v, x_sem, small_sem, first_sem, wkv_sem, wq_sem, wo_sem))

    pos_copy.start()
    for i in range(X_PARTS):
        x_part(i).start()
    g_copy.start()
    for copy in wkv_slice(0):
        copy.start()
    barrier = pltpu.get_barrier_semaphore()
    for t in range(2):
        for c in range(4):
            @pl.when((tp != t) | (cp != c))
            def _():
                pl.semaphore_signal(barrier, inc=1, device_id={"tp": t, "cp": c}, device_id_type=MESH)

    pos_copy.wait()
    for t in range(1, SLICES):
        for copy in wkv_slice(t):
            copy.start()
    rope_tables(pos_v, cos_v, sin_v)
    for i in range(X_PARTS):
        x_part(i).wait()
        if i == 1:
            wk_part(1).start()
            wv_part(1).start()
        rows = pl.ds(i * X_ROWS, X_ROWS)
        squares = None
        for t in range(WIDTH // HEAD):
            xf = out_v[rows, pl.ds(t * HEAD, HEAD)].astype(F32)
            squares = xf * xf if squares is None else squares + xf * xf
        inv_v[rows, :] = squares
    mean = jnp.sum(inv_v[...], axis=-1, keepdims=True) * (1.0 / WIDTH)
    inv_v[...] = jnp.broadcast_to(lax.rsqrt(mean + EPS), (ROWS, HEAD))
    g_copy.wait()
    gain_v[...] = g_v[...].astype(F32)

    def kv_copy(src_block, h, target, send):
        return pltpu.make_async_remote_copy(
            src_ref=kv_v.at[src_block, h], dst_ref=kv_v.at[src_block, h], send_sem=send.at[h],
            recv_sem=kv_recv.at[src_block, h], device_id={"cp": target}, device_id_type=MESH)

    def own_to(me, target, send, h):
        return kv_copy(me, h, target, send)

    def heads_of(acc, pair):
        for a in range(2):
            h = 2 * pair + a
            k = rope(acc[:, a * HEAD:(a + 1) * HEAD], cos_v[...], sin_v[...]).astype(BF16)
            kv_v[cp, h, :, pl.ds(0, HEAD)] = k
            kv_v[cp, h, :, pl.ds(HEAD, HEAD)] = acc[:, PAIR + a * HEAD:PAIR + (a + 1) * HEAD].astype(BF16)

    def send_heads(pair):
        for h in (2 * pair, 2 * pair + 1):
            @pl.when(cp == 0)
            def _():
                own_to(0, 2, kv_send, h).start()
                own_to(0, 1, kv_fwd, h).start()

            @pl.when(cp == 1)
            def _():
                own_to(1, 3, kv_send, h).start()

            @pl.when(cp == 2)
            def _():
                own_to(2, 3, kv_send, h).start()

    def query_heads(acc, j):
        for g in range(GROUP):
            q_v[j, pl.ds(g * ROWS, ROWS), :] = rope(acc[:, g * HEAD:(g + 1) * HEAD], cos_v[...], sin_v[...]).astype(BF16)

    def normalise(t):
        for u in range(NORM_COLS // HEAD):
            lanes = pl.ds(t * NORM_COLS + u * HEAD, HEAD)
            gain = gain_v[pl.ds(t * (NORM_COLS // HEAD) + u, 1), :]
            h_v[:, lanes] = (out_v[:, lanes].astype(F32) * inv_v[...] * gain).astype(BF16)

    acc = None
    normalise(0)
    for t in range(SLICES):
        cols = pl.ds(t * NORM_COLS, NORM_COLS)
        for copy in wkv_slice(t):
            copy.wait()
        if t == 1:
            wq_part(0).start()
        if t + 1 < SLICES:
            normalise(t + 1)
        d = jnp.dot(h_v[:, cols], wkv_v[0, cols, :], preferred_element_type=F32)
        acc = d if acc is None else acc + d
    wq_part(1).start()
    heads_of(acc, 0)
    pl.semaphore_wait(barrier, 7)
    send_heads(0)

    wk_part(1).wait()
    wv_part(1).wait()
    wq_part(2).start()
    pending = jnp.dot(h_v[...], wkv_v[1], preferred_element_type=F32)

    def forward(h):
        @pl.when(cp == 2)
        def _():
            kv_copy(0, h, 2, kv_send).wait_recv()
            kv_copy(0, h, 3, kv_fwd).start()

        @pl.when(cp == 3)
        def _():
            kv_copy(1, h, 3, kv_send).wait_recv()
            kv_copy(1, h, 2, kv_fwd).start()

    stats = (q_v, kv_v, o_v, max_v, sum_v, acc_v)
    for j in range(KV):
        wq_part(j).wait()
        if j == 0:
            wq_part(3).start()
        acc = jnp.dot(h_v[...], wq_v[j], preferred_element_type=F32)
        if j == 0:
            heads_of(pending, 1)
            send_heads(1)
        else:
            query_heads(pending, j - 1)
            attend_own(cp, j - 1, *stats)
        pending = acc
        for n in range(4):
            wo_part(j * 4 + n).start()
        if j == KV - 1:
            forward(0)
    query_heads(pending, KV - 1)
    attend_own(cp, KV - 1, *stats)
    forward(1)
    forward(2)

    def arrive(src_block, h):
        kv_copy(src_block, h, 0, kv_send).wait_recv()

    @pl.when(cp == 1)
    def _():
        @pl.loop(0, KV)
        def _(h):
            arrive(0, h)
            attend_earlier(0, 1, True, h, *stats)

    @pl.when(cp == 2)
    def _():
        @pl.loop(0, KV)
        def _(h):
            arrive(1, h)
            attend_earlier(0, 2, True, h, *stats)

            @pl.when(h == 1)
            def _():
                kv_copy(0, 3, 2, kv_send).wait_recv()
                kv_copy(0, 3, 3, kv_fwd).start()

    @pl.when(cp == 3)
    def _():
        @pl.loop(0, KV)
        def _(h):
            arrive(2, h)
            attend_earlier(2, 3, False, h, *stats)

            @pl.when(h == 1)
            def _():
                kv_copy(1, 3, 3, kv_send).wait_recv()
                kv_copy(1, 3, 2, kv_fwd).start()

        @pl.loop(0, KV)
        def _(h):
            arrive(0, h)
            attend_earlier(0, 2, True, h, *stats)

    def sent(n):
        return wkv_v.at[0, pl.ds(pl.multiple_of(n * ROWS, ROWS), ROWS), pl.ds(0, OCHUNK)]

    def p_copy(n):
        return pltpu.make_async_remote_copy(
            src_ref=sent(n), dst_ref=precv.at[n], send_sem=p_send.at[n], recv_sem=p_recv.at[n],
            device_id={"tp": other}, device_id_type=MESH)

    def relay_in(n):
        return pltpu.make_async_remote_copy(
            src_ref=sent(n), dst_ref=relay_v.at[n], send_sem=p_send.at[n], recv_sem=relay_recv.at[n],
            device_id={"tp": other, "cp": 1}, device_id_type=MESH)

    def relay_out(n):
        return pltpu.make_async_remote_copy(
            src_ref=relay_v.at[n], dst_ref=precv.at[n], send_sem=relay_send.at[n], recv_sem=p_recv.at[n],
            device_id={"cp": 3}, device_id_type=MESH)

    @pl.loop(0, NOUT)
    def _(n):
        wo_part(n).wait()
        room = wo_room(wq_v, n)
        part = None
        for h in range(KV):
            d = jnp.dot(o_v[h], room[pl.ds(h * QCOLS, QCOLS), :], preferred_element_type=F32)
            part = d if part is None else part + d
        sent(n)[...] = part.astype(BF16)
        detour = (cp == 3) & (n < DETOURS)

        @pl.when(detour)
        def _():
            relay_in(n).start()

        @pl.when(jnp.logical_not(detour))
        def _():
            p_copy(n).start()

    for cache, lanes in ((k_out, pl.ds(0, HEAD)), (v_out, pl.ds(HEAD, HEAD))):
        for h in range(KV):
            cache_v[pl.ds(h, ROWS, stride=KV), :] = kv_v[cp, h, :, lanes].astype(F32)
        cache[...] = cache_v[...].astype(BF16)

    for h in range(KV):
        @pl.when(cp < 3)
        def _():
            kv_copy(0, h, 0, kv_send).wait_send()

        @pl.when((cp == 0) | (cp >= 2))
        def _():
            kv_copy(0, h, 0, kv_fwd).wait_send()

    def nth(step):
        return lax.rem(step + DETOURS, NOUT)

    @pl.loop(0, NOUT)
    def _(step):
        n = nth(step)

        @pl.when(step >= LAG)
        def _():
            p_copy(nth(step - LAG)).wait_send()

        @pl.when((cp == 1) & (step == RELAY_STEP))
        def _():
            for i in range(DETOURS):
                relay_in(i).wait_recv()
                relay_out(i).start()

        @pl.when((cp == 1) & (step == NOUT - LAG))
        def _():
            for i in range(DETOURS):
                relay_out(i).wait_send()

        p_copy(n).wait_recv()
        cols = pl.ds(pl.multiple_of(n * OCHUNK, OCHUNK), OCHUNK)
        total = sent(n)[...].astype(F32) + precv[n].astype(F32)
        out_v[:, cols] = (out_v[:, cols].astype(F32) + total).astype(BF16)

    for step in range(NOUT - LAG, NOUT):
        p_copy((step + DETOURS) % NOUT).wait_send()


def store_results(out_v, k_v, v_v, out_hbm, k_hbm, v_hbm, sem):
    stores = [pltpu.make_async_copy(src, dst, sem.at[i]) for i, (src, dst) in enumerate(((out_v, out_hbm), (k_v, k_hbm), (v_v, v_hbm)))]
    for store in stores:
        store.start()
    for store in stores:
        store.wait()


def solution(mesh):
    row_spec = P(('dp', 'cp'), None)
    cache_spec = P(('dp', 'cp'), 'tp', None)
    head_cols = P(None, 'tp')

    def local_block(hidden, positions, norm_gain, w_query, w_key, w_value, w_out):
        dma = pltpu.SemaphoreType.DMA
        out, k_rope, v_heads = pl.pallas_call(
            kernel,
            out_shape=[
                jax.ShapeDtypeStruct((ROWS, WIDTH), BF16),
                jax.ShapeDtypeStruct((ROWS * KV, HEAD), BF16),
                jax.ShapeDtypeStruct((ROWS * KV, HEAD), BF16),
            ],
            in_specs=[pl.BlockSpec(memory_space=pltpu.HBM)] * 7,
            out_specs=[pl.BlockSpec(memory_space=pltpu.VMEM)] * 3,
            scratch_shapes=[
                pltpu.VMEM((ROWS,), jnp.int32),
                pltpu.VMEM((WIDTH // HEAD, HEAD), BF16),
                pltpu.VMEM((2, WIDTH, 2 * PAIR), BF16),
                pltpu.VMEM((KV, WIDTH, QCOLS), BF16),
                pltpu.VMEM((ROWS, WIDTH), BF16),
                pltpu.VMEM((WIDTH // HEAD, HEAD), F32),
                pltpu.VMEM((ROWS, HEAD), F32),
                pltpu.VMEM((ROWS, HEAD), F32),
                pltpu.VMEM((ROWS, HEAD), F32),
                pltpu.VMEM((4, KV, ROWS, 2 * HEAD), BF16),
                pltpu.VMEM((KV, GROUP * ROWS, HEAD), BF16),
                pltpu.VMEM((KV, ROWS, QCOLS), BF16),
                pltpu.VMEM((KV, 1, GROUP * ROWS), F32),
                pltpu.VMEM((KV, 1, GROUP * ROWS), F32),
                pltpu.VMEM((KV, HEAD, GROUP * ROWS), F32),
                pltpu.VMEM((NOUT, ROWS, OCHUNK), BF16),
                pltpu.VMEM((DETOURS, ROWS, OCHUNK), BF16),
                pltpu.VMEM((ROWS * KV, HEAD), F32),
                dma((X_PARTS,)), dma((2,)), dma((2, WIDTH // NORM_COLS)), dma((2, 2)), dma((KV,)), dma((NOUT,)),
                dma((KV,)), dma((KV,)), dma((4, KV)), dma((NOUT,)), dma((NOUT,)), dma((DETOURS,)), dma((DETOURS,)),
            ],
            compiler_params=pltpu.CompilerParams(collective_id=0, has_side_effects=True, vmem_limit_bytes=48 << 20),
        )(*(pltpu.with_memory_space_constraint(a, pltpu.HBM) for a in (hidden, positions, norm_gain.reshape(WIDTH // HEAD, HEAD), w_query, w_key, w_value, w_out)))
        out, k_rope, v_heads = pl.pallas_call(
            store_results,
            out_shape=[jax.ShapeDtypeStruct(a.shape, BF16) for a in (out, k_rope, v_heads)],
            in_specs=[pl.BlockSpec(memory_space=pltpu.VMEM)] * 3,
            out_specs=[pl.BlockSpec(memory_space=pl.ANY)] * 3,
            scratch_shapes=[dma((3,))],
            compiler_params=pltpu.CompilerParams(vmem_limit_bytes=4 << 20),
        )(out, k_rope, v_heads)
        return out, k_rope.reshape(ROWS, KV, HEAD), v_heads.reshape(ROWS, KV, HEAD)

    return jax.shard_map(local_block, mesh=mesh, in_specs=(row_spec, P(('dp', 'cp')), P(None), head_cols, head_cols, head_cols, P('tp', None)), out_specs=(row_spec, cache_spec, cache_spec), check_vma=False)
```

time: 74.9 us -> 68.7 us (0.917)
  Pallas kernels: 74 us -> 68 us
    pallas_call x1, Pallas kernels: 72.5 us -> 66.5 us  [local_block(): pl.pallas_call(kernel, out_shape=[jax.ShapeDtypeStruct((ROWS, WIDTH), BF1...]
where the time goes in v3:
time: 68.7 us; the launch traced here: 68.6 us
  Pallas kernels  68 us (99%)
    pallas_call x1, Pallas kernels, local_block(): pl.pallas_call(kernel, out_shape=[jax.ShapeDtypeStruct((ROWS, WIDTH), BF1...  66.5 us
    pallas_call x1, Pallas kernels, local_block(): pl.pallas_call(store_results, out_shape=[jax.ShapeDtypeStruct(a.shape, BF...  1.51 us

profile of v3, /device:TPU:3, one launch (start us, length us, event | category | flops | bytes accessed | tf_op | source)
XLA Modules:
  0.0 68.6 jit_solution(15213441065464951944)
XLA Ops:
  0.6 66.5 %shard_map.94 = (bf16[256,4096]{1,0:T(8,128)(2,1)S(1)}, bf16[1024,128]{1,0:T(8,128)(2,1)S(1)}, bf16[1024,128]{1,0:T(8,128)(2,1)S(1)}) custom-call(bf16[256,4096]{1,0:T(8,128)(2,1)} %x_hbm.1, s32[256]{0:T(256)} %pos_hbm.1, bf16[32,128]{1,0:T(8,128)(2,1)} %bitcast.3, bf16[4096,2048]{1,0:T(8,128)(2,1)} %wq_hbm.1, bf16[4096,512]{1,0:T(8,128)(2,1)} %wk_hbm.1, ...), custom_call_target="tpu_custom_call" | custom-call | tf_op jit(solution)/shard_map/pallas_call | solution.py:406
  67.1 1.5 %shard_map.95 = (bf16[256,4096]{1,0:T(8,128)(2,1)}, bf16[1024,128]{1,0:T(8,128)(2,1)}, bf16[1024,128]{1,0:T(8,128)(2,1)}) custom-call(bf16[256,4096]{1,0:T(8,128)(2,1)S(1)} %get-tuple-element.9.out_v, bf16[1024,128]{1,0:T(8,128)(2,1)S(1)} %get-tuple-element.10.k_v, bf16[1024,128]{1,0:T(8,128)(2,1)S(1)} %get-tuple-element.11.v_v), custom_call_target="tpu_custom_call" | custom-call | tf_op jit(solution)/shard_map/pallas_call | solution.py:439

commit v4 on v3

v4 whole, which is shorter than its diff:
```python
import functools
import math

import jax
import jax.numpy as jnp
from jax import lax
from jax.experimental import pallas as pl
from jax.experimental.pallas import tpu as pltpu
from jax.sharding import PartitionSpec as P

HEAD = 128
HALF = HEAD // 2
EPS = 1e-5
LOG_THETA = math.log(1000000.0)
SCORE_SCALE = 1.0 / math.sqrt(HEAD)
EXP2_SCALE = SCORE_SCALE / math.log(2.0)
MESH = pl.DeviceIdType.MESH
ROWS = 256
WIDTH = 4096
KV = 4
GROUP = 4
QCOLS = GROUP * HEAD
PAIR = 2 * HEAD
OCHUNK = 256
NOUT = WIDTH // OCHUNK
X_PARTS = 4
X_ROWS = ROWS // X_PARTS
SLICE_ROWS = 1024
SLICES = WIDTH // SLICE_ROWS
KEY_ROWS = 32
DETOUR_ROWS = (256, 128)
DETOURS = len(DETOUR_ROWS)
F32 = jnp.float32
BF16 = jnp.bfloat16


def wo_room(wq_v, n):
    deep = KV * QCOLS
    row = pl.multiple_of(lax.rem(n, 4) // 2 * deep, deep)
    col = pl.multiple_of(lax.rem(n, 2) * OCHUNK, OCHUNK)
    return wq_v.at[n // 4, pl.ds(row, deep), pl.ds(col, OCHUNK)]


def wait_bytes(room, sem):
    pltpu.make_async_copy(room, room, sem).wait()


def copies(refs):
    (x_hbm, pos_hbm, g_hbm, wq_hbm, wk_hbm, wv_hbm, wo_hbm, x_v, pos_v, g_v, wkv_v, wq_v, x_sem, small_sem, first_sem, wkv_sem, wq_sem) = refs

    def x_part(i):
        return pltpu.make_async_copy(x_hbm.at[pl.ds(i * X_ROWS, X_ROWS)], x_v.at[pl.ds(i * X_ROWS, X_ROWS)], x_sem.at[i])

    def wkv_slice(t):
        rows = pl.ds(t * SLICE_ROWS, SLICE_ROWS)
        return [pltpu.make_async_copy(w.at[rows, pl.ds(0, PAIR)], wkv_v.at[0, rows, pl.ds(a * PAIR, PAIR)], first_sem.at[t]) for a, w in enumerate((wk_hbm, wv_hbm))]

    wkv_rest = [pltpu.make_async_copy(w.at[:, pl.ds(PAIR, PAIR)], wkv_v.at[1, :, pl.ds(a * PAIR, PAIR)], wkv_sem) for a, w in enumerate((wk_hbm, wv_hbm))]

    def wq_part(j):
        return pltpu.make_async_copy(wq_hbm.at[:, pl.ds(j * QCOLS, QCOLS)], wq_v.at[j], wq_sem.at[j])

    def wo_part(j):
        deep = KV * QCOLS
        parts = []
        for a in range(2):
            cols = pl.ds(pl.multiple_of((2 * j + a) * QCOLS, QCOLS), QCOLS)
            parts.append(pltpu.make_async_copy(wo_hbm.at[:, cols], wq_v.at[j, pl.ds(a * deep, deep), :], wq_sem.at[j]))
        return parts

    pos_copy = pltpu.make_async_copy(pos_hbm, pos_v, small_sem.at[0])
    g_copy = pltpu.make_async_copy(g_hbm, g_v, small_sem.at[1])
    return x_part, wkv_slice, wkv_rest, wq_part, wo_part, pos_copy, g_copy


def rope_tables(pos_v, cos_v, sin_v):
    lane = lax.broadcasted_iota(jnp.int32, (1, HEAD), 1)
    inv_freq = jnp.exp(lax.rem(lane, HALF).astype(F32) * (-2.0 * LOG_THETA / HEAD))
    low = lane < HALF
    top = jnp.broadcast_to(pos_v[pl.ds(0, HEAD)].reshape(1, HEAD).astype(F32), (HEAD, HEAD)).T
    bottom = jnp.broadcast_to(pos_v[pl.ds(HEAD, HEAD)].reshape(1, HEAD).astype(F32), (HEAD, HEAD)).T
    angles = jnp.where(low, top, bottom) * inv_freq
    cos_t, sin_t = jnp.cos(angles), jnp.sin(angles)
    cos_r, sin_r = pltpu.roll(cos_t, HALF, 1), pltpu.roll(sin_t, HALF, 1)
    cos_v[pl.ds(0, HEAD)] = jnp.where(low, cos_t, cos_r)
    cos_v[pl.ds(HEAD, HEAD)] = jnp.where(low, cos_r, cos_t)
    sin_v[pl.ds(0, HEAD)] = jnp.where(low, -sin_t, sin_r)
    sin_v[pl.ds(HEAD, HEAD)] = jnp.where(low, -sin_r, sin_t)


def rope(vals, cos_t, sin_t):
    return vals * cos_t + pltpu.roll(vals, HALF, 1) * sin_t


def attend(units, merge, last, q_v, kv_v, o_v, max_v, sum_v, acc_v, score_v, weight_v):
    tops, sums = {}, {}

    def room(h, count):
        return h * ROWS if count <= ROWS else h % 2 * 2 * ROWS

    def score_phase(unit):
        h, start, count, first, width, causal = unit
        lanes = pl.ds(first, width)
        s = lax.dot_general(kv_v[h, pl.ds(start, count), pl.ds(0, HEAD)], q_v[h, lanes, :], (((1,), (1,)), ((), ())), preferred_element_type=F32)
        parts = [(0, s)]
        if causal:
            key = lax.broadcasted_iota(jnp.int32, (HEAD, width), 0)
            query = lax.rem(lax.broadcasted_iota(jnp.int32, (HEAD, width), 1), HEAD)
            free = count - HEAD
            parts = ([(0, s[:free])] if free else []) + [(free, jnp.where(key <= query, s[free:], -jnp.inf))]
        tall = []
        for row, part in parts:
            score_v[pl.ds(room(h, count) + row, part.shape[0]), lanes] = part
            tall.append(jnp.max(part.reshape(part.shape[0] // 8, 8, width), axis=0))
        top = jnp.max(functools.reduce(jnp.maximum, tall), axis=0, keepdims=True) * EXP2_SCALE
        tops[h, first] = jnp.maximum(top, max_v[h, :, lanes]) if merge else top

    def weight_phase(unit):
        h, start, count, first, width, causal = unit
        lanes = pl.ds(first, width)
        total = None
        for c in range(count // KEY_ROWS):
            rows = pl.ds(room(h, count) + c * KEY_ROWS, KEY_ROWS)
            w = jnp.exp2(score_v[rows, lanes] * EXP2_SCALE - tops[h, first])
            part = jnp.sum(w.reshape(KEY_ROWS // 8, 8, width), axis=0)
            total = part if total is None else total + part
            weight_v[rows, lanes] = w.astype(BF16)
        sums[h, first] = total

    def value_phase(unit):
        h, start, count, first, width, causal = unit
        lanes = pl.ds(first, width)
        acc = lax.dot_general(kv_v[h, pl.ds(start, count), pl.ds(HEAD, HEAD)], weight_v[pl.ds(room(h, count), count), lanes], (((0,), (0,)), ((), ())), preferred_element_type=F32)
        total = jnp.sum(sums[h, first], axis=0, keepdims=True)
        if merge:
            scale = jnp.exp2(max_v[h, :, lanes] - tops[h, first])
            total, acc = sum_v[h, :, lanes] * scale + total, acc_v[h, :, lanes] * scale + acc
        if not (merge and last):
            max_v[h, :, lanes], sum_v[h, :, lanes], acc_v[h, :, lanes] = tops[h, first], total, acc
        if last:
            vals = (acc / total).astype(BF16)
            for i in range(width // HEAD):
                half, g = divmod(first // HEAD + i, GROUP)
                o_v[h, pl.ds(half * HEAD, HEAD), pl.ds(g * HEAD, HEAD)] = vals[:, i * HEAD:(i + 1) * HEAD].T

    for i in range(len(units) + 2):
        if i < len(units):
            score_phase(units[i])
        if 0 <= i - 1 < len(units):
            weight_phase(units[i - 1])
        if 0 <= i - 2 < len(units):
            value_phase(units[i - 2])


def own_units(start):
    return [(h, start, (half + 1) * HEAD, half * QCOLS, QCOLS, True) for h in range(KV) for half in range(2)]


def block_units(heads, first, end):
    return [(h, first * ROWS, (end - first) * ROWS, 0, GROUP * ROWS, False) for h in heads]


def kernel(x_hbm, pos_hbm, g_hbm, wq_hbm, wk_hbm, wv_hbm, wo_hbm,
           out_v, k_out, v_out,
           pos_v, g_v, wkv_v, wq_v, h_v, gain_v, inv_v, cos_v, sin_v, kv_v, q_v, o_v, max_v, sum_v, acc_v, score_v, weight_v, precv, relay_v, cache_v,
           x_sem, small_sem, first_sem, wkv_sem, wq_sem, kv_send, kv_recv, p_send, p_recv, relay_send, relay_recv):
    tp, cp = lax.axis_index("tp"), lax.axis_index("cp")
    other = 1 - tp
    x_part, wkv_slice, wkv_rest, wq_part, wo_part, pos_copy, g_copy = copies(
        (x_hbm, pos_hbm, g_hbm, wq_hbm, wk_hbm, wv_hbm, wo_hbm, out_v, pos_v, g_v, wkv_v, wq_v, x_sem, small_sem, first_sem, wkv_sem, wq_sem))

    g_copy.start()
    for i in range(X_PARTS):
        x_part(i).start()
    pos_copy.start()
    for t in range(SLICES // 2):
        for copy in wkv_slice(t):
            copy.start()
    barrier = pltpu.get_barrier_semaphore()
    for t in range(2):
        for c in range(4):
            @pl.when((tp != t) | (cp != c))
            def _():
                pl.semaphore_signal(barrier, inc=1, device_id={"tp": t, "cp": c}, device_id_type=MESH)

    def normalise(i):
        rows = pl.ds(i * X_ROWS, X_ROWS)
        inv = inv_v[rows, :]
        for t in range(WIDTH // HEAD):
            lanes = pl.ds(t * HEAD, HEAD)
            h_v[rows, lanes] = (out_v[rows, lanes].astype(F32) * inv * gain_v[pl.ds(t, 1), :]).astype(BF16)

    g_copy.wait()
    gain_v[...] = g_v[...].astype(F32)
    for i in range(X_PARTS):
        x_part(i).wait()
        if i == 0:
            for t in range(SLICES // 2, SLICES):
                for copy in wkv_slice(t):
                    copy.start()
        if i == 3:
            for copy in wkv_rest:
                copy.start()
        rows = pl.ds(i * X_ROWS, X_ROWS)
        squares = None
        for t in range(WIDTH // HEAD):
            xf = out_v[rows, pl.ds(t * HEAD, HEAD)].astype(F32)
            squares = xf * xf if squares is None else squares + xf * xf
        mean = jnp.sum(squares, axis=-1, keepdims=True) * (1.0 / WIDTH)
        if i:
            normalise(i - 1)
        inv_v[rows, :] = jnp.broadcast_to(lax.rsqrt(mean + EPS), (X_ROWS, HEAD))
    normalise(X_PARTS - 1)

    def piece(block, h):
        return kv_v.at[h, pl.ds(pl.multiple_of(block * ROWS, ROWS), ROWS), :]

    def kv_copy(src_block, h, target):
        return pltpu.make_async_remote_copy(
            src_ref=piece(src_block, h), dst_ref=piece(src_block, h), send_sem=kv_send,
            recv_sem=kv_recv.at[src_block, h], device_id={"cp": target}, device_id_type=MESH)

    def heads_of(acc, pair):
        for a in range(2):
            h = 2 * pair + a
            k = rope(acc[:, a * HEAD:(a + 1) * HEAD], cos_v[...], sin_v[...]).astype(BF16)
            piece(cp, h)[:, pl.ds(0, HEAD)] = k
            piece(cp, h)[:, pl.ds(HEAD, HEAD)] = acc[:, PAIR + a * HEAD:PAIR + (a + 1) * HEAD].astype(BF16)

    def send_heads(pair):
        for h in (2 * pair, 2 * pair + 1):
            @pl.when(cp == 0)
            def _():
                kv_copy(0, h, 2).start()
                kv_copy(0, h, 1).start()

            @pl.when(cp == 1)
            def _():
                kv_copy(1, h, 3).start()

            @pl.when(cp == 2)
            def _():
                kv_copy(2, h, 3).start()

    def query_heads(acc, j):
        for g in range(GROUP):
            q = rope(acc[:, g * HEAD:(g + 1) * HEAD], cos_v[...], sin_v[...]).astype(BF16)
            for half in range(2):
                q_v[j, pl.ds(half * QCOLS + g * HEAD, HEAD), :] = q[half * HEAD:(half + 1) * HEAD]

    pos_copy.wait()
    acc = None
    for part in range(4):
        for t in range(part * SLICES // 4, (part + 1) * SLICES // 4):
            wait_bytes(wkv_v.at[0, pl.ds(t * SLICE_ROWS, SLICE_ROWS), :], first_sem.at[t])
        if part == 0:
            wq_part(0).start()
        deep = pl.ds(part * WIDTH // 4, WIDTH // 4)
        d = jnp.dot(h_v[:, deep], wkv_v[0, deep, :], preferred_element_type=F32)
        acc = d if acc is None else acc + d
        if part == 0:
            rope_tables(pos_v, cos_v, sin_v)
    wq_part(1).start()
    heads_of(acc, 0)
    pl.semaphore_wait(barrier, 7)
    send_heads(0)

    wait_bytes(wkv_v.at[1], wkv_sem)
    wq_part(2).start()
    pending = jnp.dot(h_v[...], wkv_v[1], preferred_element_type=F32)

    def forward_to(block, h, target):
        kv_copy(block, h, target).wait_recv()
        kv_copy(block, h, target).start()

    def forward(h):
        @pl.when(cp == 2)
        def _():
            forward_to(0, h, 3)

        @pl.when(cp == 3)
        def _():
            forward_to(1, h, 2)

    stats = (q_v, kv_v, o_v, max_v, sum_v, acc_v, score_v, weight_v)
    for j in range(KV):
        wq_part(j).wait()
        if j == 0:
            wq_part(3).start()
        acc = jnp.dot(h_v[...], wq_v[j], preferred_element_type=F32)
        if j == 0:
            heads_of(pending, 1)
            send_heads(1)
        else:
            query_heads(pending, j - 1)
        pending = acc
        for copy in wo_part(j):
            copy.start()
        if j == KV - 1:
            forward(0)
    query_heads(pending, KV - 1)
    attend(own_units(pl.multiple_of(cp * ROWS, ROWS)), False, True, *stats)
    forward(1)

    def arrive(src_block, h):
        kv_copy(src_block, h, 0).wait_recv()

    @pl.when(cp == 1)
    def _():
        for h in range(KV):
            arrive(0, h)
        attend(block_units(range(KV), 0, 1), True, True, *stats)

    @pl.when(cp == 2)
    def _():
        arrive(1, 0)
        arrive(1, 1)
        attend(block_units((0, 1), 0, 2), True, True, *stats)
        forward_to(0, 2, 3)
        arrive(1, 2)
        attend(block_units((2,), 0, 2), True, True, *stats)
        forward_to(0, 3, 3)
        arrive(1, 3)
        attend(block_units((3,), 0, 2), True, True, *stats)

    @pl.when(cp == 3)
    def _():
        for h in range(KV):
            arrive(2, h)
        attend(block_units((0, 1), 2, 3), True, False, *stats)
        forward_to(1, 2, 2)
        attend(block_units((2, 3), 2, 3), True, False, *stats)
        arrive(0, 0)
        attend(block_units((0,), 0, 2), True, True, *stats)
        forward_to(1, 3, 2)
        arrive(0, 1)
        arrive(0, 2)
        attend(block_units((1, 2), 0, 2), True, True, *stats)
        arrive(0, 3)
        attend(block_units((3,), 0, 2), True, True, *stats)

    def sent(n):
        return wkv_v.at[0, pl.ds(pl.multiple_of(n * ROWS, ROWS), ROWS), pl.ds(0, OCHUNK)]

    def group(n):
        early = (n + 2) // 4
        return jnp.where(n < 14, early, n - 10) if not isinstance(n, int) else (early if n < 14 else n - 10)

    def p_copy(n):
        return pltpu.make_async_remote_copy(
            src_ref=sent(n), dst_ref=precv.at[n], send_sem=p_send, recv_sem=p_recv.at[group(n)],
            device_id={"tp": other}, device_id_type=MESH)

    def detour(i):
        return pl.ds(0, DETOUR_ROWS[i])

    def relay_in(i):
        return pltpu.make_async_remote_copy(
            src_ref=sent(i).at[detour(i)], dst_ref=relay_v.at[pl.ds(i * ROWS, DETOUR_ROWS[i])], send_sem=p_send, recv_sem=relay_recv,
            device_id={"tp": other, "cp": 1}, device_id_type=MESH)

    def relay_out(i):
        return pltpu.make_async_remote_copy(
            src_ref=relay_v.at[pl.ds(i * ROWS, DETOUR_ROWS[i])], dst_ref=precv.at[i, detour(i)], send_sem=relay_send, recv_sem=p_recv.at[group(i)],
            device_id={"cp": 3}, device_id_type=MESH)

    def rest(i):
        rows = pl.ds(DETOUR_ROWS[i], ROWS - DETOUR_ROWS[i])
        return pltpu.make_async_remote_copy(
            src_ref=sent(i).at[rows], dst_ref=precv.at[i, rows], send_sem=p_send, recv_sem=p_recv.at[group(i)],
            device_id={"tp": other}, device_id_type=MESH)

    @pl.loop(0, NOUT)
    def _(n):
        @pl.when(lax.rem(n, 4) == 0)
        def _():
            wait_bytes(wq_v.at[n // 4], wq_sem.at[n // 4])

        room = wo_room(wq_v, n)
        part = None
        for h in range(KV):
            d = jnp.dot(o_v[h], room[pl.ds(h * QCOLS, QCOLS), :], preferred_element_type=F32)
            part = d if part is None else part + d
        sent(n)[...] = part.astype(BF16)
        for i in range(DETOURS):
            @pl.when((cp == 3) & (n == i))
            def _():
                relay_in(i).start()
                if DETOUR_ROWS[i] < ROWS:
                    rest(i).start()

        @pl.when((cp < 3) | (n >= DETOURS))
        def _():
            p_copy(n).start()

    for cache, lanes in ((k_out, pl.ds(0, HEAD)), (v_out, pl.ds(HEAD, HEAD))):
        for h in range(KV):
            cache_v[pl.ds(h, ROWS, stride=KV), :] = piece(cp, h)[:, lanes].astype(F32)
        cache[...] = cache_v[...].astype(BF16)

    @pl.when(lax.rem(cp, 2) == 0)
    def _():
        wait_bytes(kv_v.at[:, pl.ds(0, 2 * ROWS), :], kv_send)

    @pl.when(lax.rem(cp, 2) == 1)
    def _():
        wait_bytes(kv_v.at[:, pl.ds(0, ROWS), :], kv_send)

    def add_chunks(first, count):
        wait_bytes(precv.at[pl.ds(first, count)], p_recv.at[group(first)])
        for n in range(first, first + count):
            cols = pl.ds(n * OCHUNK, OCHUNK)
            total = sent(n)[...].astype(F32) + precv[n].astype(F32)
            out_v[:, cols] = (out_v[:, cols].astype(F32) + total).astype(BF16)

    add_chunks(2, 4)
    add_chunks(6, 4)

    @pl.when(cp == 1)
    def _():
        wait_bytes(relay_v, relay_recv)
        for i in range(DETOURS):
            relay_out(i).start()

    add_chunks(10, 4)

    @pl.when(cp == 1)
    def _():
        wait_bytes(relay_v, relay_send)

    add_chunks(0, 2)
    add_chunks(14, 1)
    add_chunks(15, 1)
    wait_bytes(precv, p_send)


def store_results(out_v, k_v, v_v, out_hbm, k_hbm, v_hbm, sem):
    stores = [pltpu.make_async_copy(src, dst, sem.at[i]) for i, (src, dst) in enumerate(((out_v, out_hbm), (k_v, k_hbm), (v_v, v_hbm)))]
    for store in stores:
        store.start()
    for store in stores:
        store.wait()


def solution(mesh):
    row_spec = P(('dp', 'cp'), None)
    cache_spec = P(('dp', 'cp'), 'tp', None)
    head_cols = P(None, 'tp')

    def local_block(hidden, positions, norm_gain, w_query, w_key, w_value, w_out):
        dma = pltpu.SemaphoreType.DMA
        out, k_rope, v_heads = pl.pallas_call(
            kernel,
            out_shape=[
                jax.ShapeDtypeStruct((ROWS, WIDTH), BF16),
                jax.ShapeDtypeStruct((ROWS * KV, HEAD), BF16),
                jax.ShapeDtypeStruct((ROWS * KV, HEAD), BF16),
            ],
            in_specs=[pl.BlockSpec(memory_space=pltpu.HBM)] * 7,
            out_specs=[pl.BlockSpec(memory_space=pltpu.VMEM)] * 3,
            scratch_shapes=[
                pltpu.VMEM((ROWS,), jnp.int32),
                pltpu.VMEM((WIDTH // HEAD, HEAD), BF16),
                pltpu.VMEM((2, WIDTH, 2 * PAIR), BF16),
                pltpu.VMEM((KV, WIDTH, QCOLS), BF16),
                pltpu.VMEM((ROWS, WIDTH), BF16),
                pltpu.VMEM((WIDTH // HEAD, HEAD), F32),
                pltpu.VMEM((ROWS, HEAD), F32),
                pltpu.VMEM((ROWS, HEAD), F32),
                pltpu.VMEM((ROWS, HEAD), F32),
                pltpu.VMEM((KV, 4 * ROWS, 2 * HEAD), BF16),
                pltpu.VMEM((KV, GROUP * ROWS, HEAD), BF16),
                pltpu.VMEM((KV, ROWS, QCOLS), BF16),
                pltpu.VMEM((KV, 1, GROUP * ROWS), F32),
                pltpu.VMEM((KV, 1, GROUP * ROWS), F32),
                pltpu.VMEM((KV, HEAD, GROUP * ROWS), F32),
                pltpu.VMEM((KV * ROWS, GROUP * ROWS), F32),
                pltpu.VMEM((KV * ROWS, GROUP * ROWS), BF16),
                pltpu.VMEM((NOUT, ROWS, OCHUNK), BF16),
                pltpu.VMEM((sum(DETOUR_ROWS), OCHUNK), BF16),
                pltpu.VMEM((ROWS * KV, HEAD), F32),
                dma((X_PARTS,)), dma((2,)), dma((SLICES,)), dma, dma((KV,)),
                dma, dma((3, KV)), dma, dma((6,)), dma, dma,
            ],
            compiler_params=pltpu.CompilerParams(collective_id=0, has_side_effects=True, vmem_limit_bytes=49 << 20),
        )(*(pltpu.with_memory_space_constraint(a, pltpu.HBM) for a in (hidden, positions, norm_gain.reshape(WIDTH // HEAD, HEAD), w_query, w_key, w_value, w_out)))
        out, k_rope, v_heads = pl.pallas_call(
            store_results,
            out_shape=[jax.ShapeDtypeStruct(a.shape, BF16) for a in (out, k_rope, v_heads)],
            in_specs=[pl.BlockSpec(memory_space=pltpu.VMEM)] * 3,
            out_specs=[pl.BlockSpec(memory_space=pl.ANY)] * 3,
            scratch_shapes=[dma((3,))],
            compiler_params=pltpu.CompilerParams(vmem_limit_bytes=4 << 20),
        )(out, k_rope, v_heads)
        return out, k_rope.reshape(ROWS, KV, HEAD), v_heads.reshape(ROWS, KV, HEAD)

    return jax.shard_map(local_block, mesh=mesh, in_specs=(row_spec, P(('dp', 'cp')), P(None), head_cols, head_cols, head_cols, P('tp', None)), out_specs=(row_spec, cache_spec, cache_spec), check_vma=False)
```

time: 68.7 us -> 67.2 us (0.978)
  Pallas kernels: 68 us -> 65.7 us
    pallas_call x1, Pallas kernels: 66.5 us -> 64.2 us  [local_block(): pl.pallas_call(kernel, out_shape=[jax.ShapeDtypeStruct((ROWS, WIDTH), BF1...]
where the time goes in v4:
time: 67.2 us; the launch traced here: 66.5 us
  Pallas kernels  65.7 us (98%)
  between operations  0.8 us (1%)
    pallas_call x1, Pallas kernels, local_block(): pl.pallas_call(kernel, out_shape=[jax.ShapeDtypeStruct((ROWS, WIDTH), BF1...  64.2 us
    pallas_call x1, Pallas kernels, local_block(): pl.pallas_call(store_results, out_shape=[jax.ShapeDtypeStruct(a.shape, BF...  1.51 us

profile of v4, /device:TPU:3, one launch (start us, length us, event | category | flops | bytes accessed | tf_op | source)
XLA Modules:
  0.0 66.5 jit_solution(10295328173698178560)
XLA Ops:
  0.6 64.2 %shard_map.94 = (bf16[256,4096]{1,0:T(8,128)(2,1)S(1)}, bf16[1024,128]{1,0:T(8,128)(2,1)S(1)}, bf16[1024,128]{1,0:T(8,128)(2,1)S(1)}) custom-call(bf16[256,4096]{1,0:T(8,128)(2,1)} %x_hbm.1, s32[256]{0:T(256)} %pos_hbm.1, bf16[32,128]{1,0:T(8,128)(2,1)} %bitcast.3, bf16[4096,2048]{1,0:T(8,128)(2,1)} %wq_hbm.1, bf16[4096,512]{1,0:T(8,128)(2,1)} %wk_hbm.1, ...), custom_call_target="tpu_custom_call" | custom-call | tf_op jit(solution)/shard_map/pallas_call | solution.py:452
  64.8 1.5 %shard_map.95 = (bf16[256,4096]{1,0:T(8,128)(2,1)}, bf16[1024,128]{1,0:T(8,128)(2,1)}, bf16[1024,128]{1,0:T(8,128)(2,1)}) custom-call(bf16[256,4096]{1,0:T(8,128)(2,1)S(1)} %get-tuple-element.9.out_v, bf16[1024,128]{1,0:T(8,128)(2,1)S(1)} %get-tuple-element.10.k_v, bf16[1024,128]{1,0:T(8,128)(2,1)S(1)} %get-tuple-element.11.v_v), custom_call_target="tpu_custom_call" | custom-call | tf_op jit(solution)/shard_map/pallas_call | solution.py:487

commit v5 on v4

--- a/solution.py
+++ b/solution.py
@@ -28,8 +28,7 @@
 SLICE_ROWS = 1024
 SLICES = WIDTH // SLICE_ROWS
 KEY_ROWS = 32
-DETOUR_ROWS = (256, 128)
-DETOURS = len(DETOUR_ROWS)
+DETOUR_ROWS = {1: (256, 256, 256), 3: (256, 256, 256)}
 F32 = jnp.float32
 BF16 = jnp.bfloat16
 
@@ -343,7 +342,7 @@
         return wkv_v.at[0, pl.ds(pl.multiple_of(n * ROWS, ROWS), ROWS), pl.ds(0, OCHUNK)]
 
     def group(n):
-        early = (n + 2) // 4
+        early = (n + 1) // 4
         return jnp.where(n < 14, early, n - 10) if not isinstance(n, int) else (early if n < 14 else n - 10)
 
     def p_copy(n):
@@ -351,24 +350,32 @@
             src_ref=sent(n), dst_ref=precv.at[n], send_sem=p_send, recv_sem=p_recv.at[group(n)],
             device_id={"tp": other}, device_id_type=MESH)
 
-    def detour(i):
-        return pl.ds(0, DETOUR_ROWS[i])
-
-    def relay_in(i):
+    def held(me, i):
+        return pl.ds(sum(DETOUR_ROWS[me][:i]), DETOUR_ROWS[me][i])
+
+    def relay_in(me, i):
         return pltpu.make_async_remote_copy(
-            src_ref=sent(i).at[detour(i)], dst_ref=relay_v.at[pl.ds(i * ROWS, DETOUR_ROWS[i])], send_sem=p_send, recv_sem=relay_recv,
-            device_id={"tp": other, "cp": 1}, device_id_type=MESH)
-
-    def relay_out(i):
+            src_ref=sent(i).at[pl.ds(0, DETOUR_ROWS[me][i])], dst_ref=relay_v.at[held(me, i)], send_sem=p_send, recv_sem=relay_recv,
+            device_id={"tp": other, "cp": 4 - me}, device_id_type=MESH)
+
+    def relay_out(me, i):
         return pltpu.make_async_remote_copy(
-            src_ref=relay_v.at[pl.ds(i * ROWS, DETOUR_ROWS[i])], dst_ref=precv.at[i, detour(i)], send_sem=relay_send, recv_sem=p_recv.at[group(i)],
-            device_id={"cp": 3}, device_id_type=MESH)
-
-    def rest(i):
-        rows = pl.ds(DETOUR_ROWS[i], ROWS - DETOUR_ROWS[i])
+            src_ref=relay_v.at[held(me, i)], dst_ref=precv.at[i, pl.ds(0, DETOUR_ROWS[me][i])], send_sem=relay_send, recv_sem=p_recv.at[group(i)],
+            device_id={"cp": me}, device_id_type=MESH)
+
+    def rest(me, i):
+        rows = pl.ds(DETOUR_ROWS[me][i], ROWS - DETOUR_ROWS[me][i])
         return pltpu.make_async_remote_copy(
             src_ref=sent(i).at[rows], dst_ref=precv.at[i, rows], send_sem=p_send, recv_sem=p_recv.at[group(i)],
             device_id={"tp": other}, device_id_type=MESH)
+
+    def pass_on(me):
+        wait_bytes(relay_v.at[pl.ds(0, sum(DETOUR_ROWS[me]))], relay_recv)
+        for i in range(len(DETOUR_ROWS[me])):
+            relay_out(me, i).start()
+
+    def passed_on(me):
+        wait_bytes(relay_v.at[pl.ds(0, sum(DETOUR_ROWS[me]))], relay_send)
 
     @pl.loop(0, NOUT)
     def _(n):
@@ -382,16 +389,25 @@
             d = jnp.dot(o_v[h], room[pl.ds(h * QCOLS, QCOLS), :], preferred_element_type=F32)
             part = d if part is None else part + d
         sent(n)[...] = part.astype(BF16)
-        for i in range(DETOURS):
-            @pl.when((cp == 3) & (n == i))
-            def _():
-                relay_in(i).start()
-                if DETOUR_ROWS[i] < ROWS:
-                    rest(i).start()
-
-        @pl.when((cp < 3) | (n >= DETOURS))
+        for me, detours in DETOUR_ROWS.items():
+            for i in range(len(detours)):
+                @pl.when((cp == me) & (n == i))
+                def _():
+                    relay_in(me, i).start()
+                    if detours[i] < ROWS:
+                        rest(me, i).start()
+
+        direct = lax.rem(cp, 2) == 0
+        for me, detours in DETOUR_ROWS.items():
+            direct = direct | ((cp == me) & (n >= len(detours)))
+
+        @pl.when(direct)
         def _():
             p_copy(n).start()
+
+    @pl.when(cp == 3)
+    def _():
+        pass_on(1)
 
     for cache, lanes in ((k_out, pl.ds(0, HEAD)), (v_out, pl.ds(HEAD, HEAD))):
         for h in range(KV):
@@ -413,22 +429,24 @@
             total = sent(n)[...].astype(F32) + precv[n].astype(F32)
             out_v[:, cols] = (out_v[:, cols].astype(F32) + total).astype(BF16)
 
-    add_chunks(2, 4)
-    add_chunks(6, 4)
+    add_chunks(3, 4)
+    add_chunks(7, 4)
 
     @pl.when(cp == 1)
     def _():
-        wait_bytes(relay_v, relay_recv)
-        for i in range(DETOURS):
-            relay_out(i).start()
-
-    add_chunks(10, 4)
+        pass_on(3)
+
+    @pl.when(cp == 3)
+    def _():
+        passed_on(1)
+
+    add_chunks(11, 3)
 
     @pl.when(cp == 1)
     def _():
-        wait_bytes(relay_v, relay_send)
-
-    add_chunks(0, 2)
+        passed_on(3)
+
+    add_chunks(0, 3)
     add_chunks(14, 1)
     add_chunks(15, 1)
     wait_bytes(precv, p_send)
@@ -477,7 +495,7 @@
                 pltpu.VMEM((KV * ROWS, GROUP * ROWS), F32),
                 pltpu.VMEM((KV * ROWS, GROUP * ROWS), BF16),
                 pltpu.VMEM((NOUT, ROWS, OCHUNK), BF16),
-                pltpu.VMEM((sum(DETOUR_ROWS), OCHUNK), BF16),
+                pltpu.VMEM((max(map(sum, DETOUR_ROWS.values())), OCHUNK), BF16),
                 pltpu.VMEM((ROWS * KV, HEAD), F32),
                 dma((X_PARTS,)), dma((2,)), dma((SLICES,)), dma, dma((KV,)),
                 dma, dma((3, KV)), dma, dma((6,)), dma, dma,

time: 67.2 us -> 65.9 us (0.981)
  the two profiles are of different devices: /device:TPU:3 before, /device:TPU:0 now
where the time goes in v5:
time: 65.9 us; the launch traced here: 65.8 us
  Pallas kernels  65 us (99%)
  between operations  0.8 us (1%)
    pallas_call x1, Pallas kernels, local_block(): pl.pallas_call(kernel, out_shape=[jax.ShapeDtypeStruct((ROWS, WIDTH), BF1...  63.5 us
    pallas_call x1, Pallas kernels, local_block(): pl.pallas_call(store_results, out_shape=[jax.ShapeDtypeStruct(a.shape, BF...  1.51 us

profile of v5, /device:TPU:0, one launch (start us, length us, event | category | flops | bytes accessed | tf_op | source)
XLA Modules:
  0.0 65.8 jit_solution(12148371819249984058)
XLA Ops:
  0.6 63.5 %shard_map.94 = (bf16[256,4096]{1,0:T(8,128)(2,1)S(1)}, bf16[1024,128]{1,0:T(8,128)(2,1)S(1)}, bf16[1024,128]{1,0:T(8,128)(2,1)S(1)}) custom-call(bf16[256,4096]{1,0:T(8,128)(2,1)} %x_hbm.1, s32[256]{0:T(256)} %pos_hbm.1, bf16[32,128]{1,0:T(8,128)(2,1)} %bitcast.3, bf16[4096,2048]{1,0:T(8,128)(2,1)} %wq_hbm.1, bf16[4096,512]{1,0:T(8,128)(2,1)} %wk_hbm.1, ...), custom_call_target="tpu_custom_call" | custom-call | tf_op jit(solution)/shard_map/pallas_call | solution.py:470
  64.1 1.5 %shard_map.95 = (bf16[256,4096]{1,0:T(8,128)(2,1)}, bf16[1024,128]{1,0:T(8,128)(2,1)}, bf16[1024,128]{1,0:T(8,128)(2,1)}) custom-call(bf16[256,4096]{1,0:T(8,128)(2,1)S(1)} %get-tuple-element.9.out_v, bf16[1024,128]{1,0:T(8,128)(2,1)S(1)} %get-tuple-element.10.k_v, bf16[1024,128]{1,0:T(8,128)(2,1)S(1)} %get-tuple-element.11.v_v), custom_call_target="tpu_custom_call" | custom-call | tf_op jit(solution)/shard_map/pallas_call | solution.py:505

commit v6 on v5

--- a/solution.py
+++ b/solution.py
@@ -28,7 +28,7 @@
 SLICE_ROWS = 1024
 SLICES = WIDTH // SLICE_ROWS
 KEY_ROWS = 32
-DETOUR_ROWS = {1: (256, 256, 256), 3: (256, 256, 256)}
+DETOUR_ROWS = {1: (256, 256, 256), 3: (256, 256, 192)}
 F32 = jnp.float32
 BF16 = jnp.bfloat16
 
@@ -172,7 +172,7 @@
     for i in range(X_PARTS):
         x_part(i).start()
     pos_copy.start()
-    for t in range(SLICES // 2):
+    for t in range(1):
         for copy in wkv_slice(t):
             copy.start()
     barrier = pltpu.get_barrier_semaphore()
@@ -194,7 +194,7 @@
     for i in range(X_PARTS):
         x_part(i).wait()
         if i == 0:
-            for t in range(SLICES // 2, SLICES):
+            for t in range(1, SLICES):
                 for copy in wkv_slice(t):
                     copy.start()
         if i == 3:

time: 65.9 us -> 65.6 us (level)
  the two profiles are of different devices: /device:TPU:0 before, /device:TPU:2 now
where the time goes in v6:
time: 65.6 us; the launch traced here: 65.5 us
  Pallas kernels  64.7 us (99%)
  between operations  0.8 us (1%)
    pallas_call x1, Pallas kernels, local_block(): pl.pallas_call(kernel, out_shape=[jax.ShapeDtypeStruct((ROWS, WIDTH), BF1...  63.2 us
    pallas_call x1, Pallas kernels, local_block(): pl.pallas_call(store_results, out_shape=[jax.ShapeDtypeStruct(a.shape, BF...  1.51 us

profile of v6, /device:TPU:2, one launch (start us, length us, event | category | flops | bytes accessed | tf_op | source)
XLA Modules:
  0.0 65.5 jit_solution(264556160952633484)
XLA Ops:
  0.6 63.2 %shard_map.94 = (bf16[256,4096]{1,0:T(8,128)(2,1)S(1)}, bf16[1024,128]{1,0:T(8,128)(2,1)S(1)}, bf16[1024,128]{1,0:T(8,128)(2,1)S(1)}) custom-call(bf16[256,4096]{1,0:T(8,128)(2,1)} %x_hbm.1, s32[256]{0:T(256)} %pos_hbm.1, bf16[32,128]{1,0:T(8,128)(2,1)} %bitcast.3, bf16[4096,2048]{1,0:T(8,128)(2,1)} %wq_hbm.1, bf16[4096,512]{1,0:T(8,128)(2,1)} %wk_hbm.1, ...), custom_call_target="tpu_custom_call" | custom-call | tf_op jit(solution)/shard_map/pallas_call | solution.py:470
  63.8 1.5 %shard_map.95 = (bf16[256,4096]{1,0:T(8,128)(2,1)}, bf16[1024,128]{1,0:T(8,128)(2,1)}, bf16[1024,128]{1,0:T(8,128)(2,1)}) custom-call(bf16[256,4096]{1,0:T(8,128)(2,1)S(1)} %get-tuple-element.9.out_v, bf16[1024,128]{1,0:T(8,128)(2,1)S(1)} %get-tuple-element.10.k_v, bf16[1024,128]{1,0:T(8,128)(2,1)S(1)} %get-tuple-element.11.v_v), custom_call_target="tpu_custom_call" | custom-call | tf_op jit(solution)/shard_map/pallas_call | solution.py:505

commit v7 on v6

--- a/solution.py
+++ b/solution.py
@@ -28,7 +28,7 @@
 SLICE_ROWS = 1024
 SLICES = WIDTH // SLICE_ROWS
 KEY_ROWS = 32
-DETOUR_ROWS = {1: (256, 256, 256), 3: (256, 256, 192)}
+DETOUR_ROWS = {1: (256, 256, 256), 3: (256, 256, 208)}
 F32 = jnp.float32
 BF16 = jnp.bfloat16
 
@@ -197,7 +197,7 @@
             for t in range(1, SLICES):
                 for copy in wkv_slice(t):
                     copy.start()
-        if i == 3:
+        if i == 2:
             for copy in wkv_rest:
                 copy.start()
         rows = pl.ds(i * X_ROWS, X_ROWS)

time: 65.6 us -> 65.5 us (level)
  no operation moved by 1% of the time
where the time goes in v7:
time: 65.5 us; the launch traced here: 65.4 us
  Pallas kernels  64.6 us (99%)
  between operations  0.8 us (1%)
    pallas_call x1, Pallas kernels, local_block(): pl.pallas_call(kernel, out_shape=[jax.ShapeDtypeStruct((ROWS, WIDTH), BF1...  63.1 us
    pallas_call x1, Pallas kernels, local_block(): pl.pallas_call(store_results, out_shape=[jax.ShapeDtypeStruct(a.shape, BF...  1.51 us

profile of v7, /device:TPU:2, one launch (start us, length us, event | category | flops | bytes accessed | tf_op | source)
XLA Modules:
  0.0 65.4 jit_solution(15184559300765498854)
XLA Ops:
  0.6 63.1 %shard_map.94 = (bf16[256,4096]{1,0:T(8,128)(2,1)S(1)}, bf16[1024,128]{1,0:T(8,128)(2,1)S(1)}, bf16[1024,128]{1,0:T(8,128)(2,1)S(1)}) custom-call(bf16[256,4096]{1,0:T(8,128)(2,1)} %x_hbm.1, s32[256]{0:T(256)} %pos_hbm.1, bf16[32,128]{1,0:T(8,128)(2,1)} %bitcast.3, bf16[4096,2048]{1,0:T(8,128)(2,1)} %wq_hbm.1, bf16[4096,512]{1,0:T(8,128)(2,1)} %wk_hbm.1, ...), custom_call_target="tpu_custom_call" | custom-call | tf_op jit(solution)/shard_map/pallas_call | solution.py:470
  63.7 1.5 %shard_map.95 = (bf16[256,4096]{1,0:T(8,128)(2,1)}, bf16[1024,128]{1,0:T(8,128)(2,1)}, bf16[1024,128]{1,0:T(8,128)(2,1)}) custom-call(bf16[256,4096]{1,0:T(8,128)(2,1)S(1)} %get-tuple-element.9.out_v, bf16[1024,128]{1,0:T(8,128)(2,1)S(1)} %get-tuple-element.10.k_v, bf16[1024,128]{1,0:T(8,128)(2,1)S(1)} %get-tuple-element.11.v_v), custom_call_target="tpu_custom_call" | custom-call | tf_op jit(solution)/shard_map/pallas_call | solution.py:505
